TPU v7x, 32 devices: a whole 2x2x4 slice. The times are simulated.
32 devices in a mesh: branch: 4 (over z), row: 4 (over y, x), col: 2 (over core).
Axes of the slice: x: 2, y: 2, z: 4, core: 2. Of those that a mesh axis runs over, the one named last changes fastest.
Arguments:
- section_in: bfloat16 [4, 4, 2, 48, 4096], P('branch', 'row', 'col'), may hold values from -6 to 6
- conv_weight: bfloat16 [4, 2, 3, 3, 384, 384], P('branch'), may hold values from -1 to 1, as said below
- conv_bias: float32 [4, 2, 384], P('branch'), may hold values from -3 to 3
- join_weight: bfloat16 [720, 720], replicated, may hold values from -0.4375 to 0.4375
- join_bias: float32 [720], replicated, may hold values from -3 to 3
Outputs:
- joined_first: bfloat16 [48, 128, 256], P(None, ('branch', 'row'), 'col')
- joined_second: bfloat16 [96, 64, 128], P(None, ('branch', 'row'), 'col')
- joined_third: bfloat16 [192, 32, 64], P(None, ('branch', 'row'), 'col')
- joined_fourth: bfloat16 [384, 16, 32], P(None, ('branch', 'row'), 'col')
Inputs may be any that keep to these rules, and one draw needn't show every extreme that they name: `conv_weight`: entries of branch b's kernels have standard deviation (9 * 2^b * 48) ** -0.5; entries outside the C_b x C_b corner are drawn too and unused.
All inputs are finite; a program needn't handle non-finite values.
Results may differ from a plain program's by a relative error of at most 0.0075.
Values may be sent and summed in bfloat16 or wider, within the bound.
A program may use at most 128 MiB of HBM per device.

v0:
```python
from functools import partial

import jax
import jax.numpy as jnp
from jax import lax
from jax.experimental import pallas as pl
from jax.experimental.pallas import tpu as pltpu
from jax.sharding import PartitionSpec as P

WIDTH = 48
TH = 32
TW = 128


def row_pitch(branch_level):
    return 2 * TW >> branch_level


def natural_tile(branch_level, container_ref):
    pixels = TH * TW >> 2 * branch_level
    if branch_level == 0:
        return container_ref[...].astype(jnp.float32)
    channels = WIDTH << branch_level
    parts = []
    for part in range(1 << branch_level):
        at = part * pixels
        low = at // LANES * LANES
        piece = container_ref[:, low : low + max(pixels, LANES)]
        if at > low:
            piece = pltpu.roll(piece.astype(jnp.float32), LANES - at + low, 1).astype(jnp.bfloat16)
        parts.append(piece)
    held = lax.broadcasted_iota(jnp.int32, (1, channels), 1)
    part = sum((held >= WIDTH * turn).astype(jnp.int32) for turn in range(1, 1 << branch_level))
    home = ((held - WIDTH * part) << branch_level) + part
    order = jnp.where(lax.broadcasted_iota(jnp.int32, (channels, channels), 0) == home, 1.0, 0.0)
    return jnp.dot(
        order.astype(jnp.bfloat16),
        jnp.concatenate(parts, axis=0),
        preferred_element_type=jnp.float32,
    )


def turned(group, shift):
    shift = shift % LANES
    return pltpu.roll(group, shift, 1) if shift else group


def halo_kernel(
    container_ref, ext0, ext1, ext2, ext3, row_send, row_recv, col_send, col_recv, send_sem, recv_sem
):
    level = lax.axis_index("branch")
    place = lax.axis_index("row")
    col = lax.axis_index("col")
    row_count = lax.axis_size("row")
    col_count = lax.axis_size("col")
    up, down = place > 0, place < row_count - 1
    left, right = col > 0, col < col_count - 1
    above = (level, lax.rem(place + row_count - 1, row_count), col)
    below = (level, lax.rem(place + 1, row_count), col)
    west = (level, place, lax.rem(col + col_count - 1, col_count))
    east = (level, place, lax.rem(col + 1, col_count))
    neighbours = ((up, above), (down, below), (left, west), (right, east))

    barrier = pltpu.get_barrier_semaphore()
    for exists, device in neighbours:

        @pl.when(exists)
        def _():
            pl.semaphore_signal(barrier, inc=1, device_id=device, device_id_type=MESH)

    pl.semaphore_wait(barrier, sum(exists.astype(jnp.int32) for exists, _ in neighbours))

    def side_copy(rows, way):
        source, target = (row_send, row_recv) if way < 2 else (col_send, col_recv)
        return pltpu.make_async_remote_copy(
            src_ref=source.at[way % 2, 0:rows],
            dst_ref=target.at[1 - way % 2, 0:rows],
            send_sem=send_sem.at[way],
            recv_sem=recv_sem.at[way],
            device_id=neighbours[way][1],
            device_id_type=MESH,
        )

    lane = lax.broadcasted_iota(jnp.int32, (1, LANES), 1)

    def swap(rows, first_way):
        for way in (first_way, first_way + 1):

            @pl.when(neighbours[way][0])
            def _():
                side_copy(rows, way).start()

        received = row_recv if first_way == 0 else col_recv
        for way in (first_way, first_way + 1):
            exists = neighbours[first_way + 1 - way % 2][0]

            @pl.when(exists)
            def _():
                side_copy(rows, way).wait_recv()

            @pl.when(jnp.logical_not(exists))
            def _():
                received[1 - way % 2, 0:rows] = jnp.zeros((rows, LANES), jnp.bfloat16)

    def extend(branch_level, out_ref):
        channels, total = out_ref.shape
        rows, cols, pitch = TH >> branch_level, TW >> branch_level, row_pitch(branch_level)
        apart = cols * 2 >= LANES
        tile = natural_tile(branch_level, container_ref)

        def tile_row(y):
            at = y * cols
            low = at // LANES * LANES
            return tile[:, low : low + LANES], at - low

        for side, first in enumerate((0, rows - 2)):
            if apart:
                for turn in range(2):
                    group, at = tile_row(first + turn)
                    row_send[side, turn * channels : (turn + 1) * channels] = turned(
                        group, -at
                    ).astype(jnp.bfloat16)
            else:
                group, at = tile_row(first)
                row_send[side, 0:channels] = turned(group, -at).astype(jnp.bfloat16)
        swap(2 * channels if apart else channels, 0)

        def wide_row(r):
            if 2 <= r < rows + 2:
                return tile_row(r - 2)
            side, turn = (0, r) if r < 2 else (1, r - rows - 2)
            if apart:
                group = row_recv[side, turn * channels : (turn + 1) * channels]
                return group.astype(jnp.float32), 0
            return row_recv[side, 0:channels].astype(jnp.float32), turn * cols

        firsts = jnp.zeros((channels, LANES), jnp.float32)
        lasts = firsts
        for r in range(rows + 4):
            group, at = wide_row(r)
            here = lax.shift_right_logical(lane, 1) == r
            firsts = jnp.where(here, turned(group, 2 * r - at), firsts)
            lasts = jnp.where(here, turned(group, 2 * r - at - cols + 2), lasts)
        col_send[0, 0:channels] = firsts.astype(jnp.bfloat16)
        col_send[1, 0:channels] = lasts.astype(jnp.bfloat16)
        swap(channels, 2)
        from_west = col_recv[0, 0:channels].astype(jnp.float32)
        from_east = col_recv[1, 0:channels].astype(jnp.float32)

        groups = [None] * (total // LANES)

        def put(start, count, group, at):
            index, low = start // LANES, start % LANES
            group = turned(group, low - at)
            held = 0.0 if groups[index] is None else groups[index]
            groups[index] = (
                group
                if count == LANES
                else jnp.where((lane >= low) & (lane < low + count), group, held)
            )

        for r in range(rows + 4):
            put(r * pitch, cols, *wide_row(r))
            put(r * pitch + cols, 2, from_east, 2 * r)
            put((r - 1) % (rows + 4) * pitch + pitch - 2, 2, from_west, 2 * r)
        for index, group in enumerate(groups):
            out_ref[:, index * LANES : (index + 1) * LANES] = group.astype(jnp.bfloat16)

        for first_way, count in ((0, 2 * channels if apart else channels), (2, channels)):
            for way in (first_way, first_way + 1):

                @pl.when(neighbours[way][0])
                def _():
                    side_copy(count, way).wait_send()

    for branch_level, out_ref in enumerate((ext0, ext1, ext2, ext3)):
        pl.when(level == branch_level)(partial(extend, branch_level, out_ref))


def extended_tiles(container):
    vmem = pl.BlockSpec(memory_space=pltpu.VMEM)
    side = pltpu.VMEM((2, 8 * WIDTH, LANES), jnp.bfloat16)
    return pl.pallas_call(
        halo_kernel,
        out_shape=[
            jax.ShapeDtypeStruct((WIDTH << b, ((TH >> b) + 4) * row_pitch(b)), jnp.bfloat16)
            for b in range(4)
        ],
        in_specs=[vmem],
        out_specs=[vmem] * 4,
        scratch_shapes=[
            side,
            side,
            side,
            side,
            pltpu.SemaphoreType.DMA((4,)),
            pltpu.SemaphoreType.DMA((4,)),
        ],
        compiler_params=pltpu.CompilerParams(collective_id=1, has_side_effects=True),
        name="halo",
    )(container)


def tap_stack(field, pitch, rows_kept):
    total = field.shape[1]
    views = {}
    for dx in (-1, 0, 1):
        if pitch % LANES == 0:
            view = field if dx == 0 else pltpu.roll(field, -dx % total, 1)
            view = view.astype(jnp.bfloat16)
            if rows_kept:
                step = LANES
                view = jnp.concatenate(
                    [view[:, y * pitch : y * pitch + LANES] for y in range(1, rows_kept + 3)],
                    axis=1,
                )
                size = rows_kept * LANES
            else:
                step = pitch
                view = jnp.concatenate([view[:, total - pitch :], view, view[:, :pitch]], axis=1)
                size = total
            for dy in range(3):
                views[dy, dx] = view[:, dy * step : dy * step + size]
        else:
            for dy in range(3):
                shift = -(dx + (dy - 1) * pitch) % total
                view = field if shift == 0 else pltpu.roll(field, shift, 1)
                views[dy, dx] = view.astype(jnp.bfloat16)
    return jnp.concatenate([views[dy, dx] for dy in range(3) for dx in (-1, 0, 1)], axis=0)


def taps_of(weight_refs, layer):
    if len(weight_refs) == 2:
        return weight_refs[layer][...]
    (weight_ref,) = weight_refs
    return jnp.concatenate(
        [weight_ref[layer, dy, dx] for dy in range(3) for dx in range(3)], axis=1
    )


def folded(group, pixels):
    folds = LANES // pixels
    size = group.shape[0] // folds
    lane = lax.broadcasted_iota(jnp.int32, (1, LANES), 1)
    merged = group[:size]
    for turn in range(1, folds):
        part = turned(group[turn * size : (turn + 1) * size], turn * pixels)
        merged = jnp.where(lane < turn * pixels, merged, part)
    return [merged]


def block_kernel(branch_level, ext_ref, bias_ref, *refs):
    weight_refs, strips_ref = refs[:-1], refs[-1]
    pitch = row_pitch(branch_level)
    tile_rows, tile_cols = TH >> branch_level, TW >> branch_level
    channels, total = ext_ref.shape
    place, col = lax.axis_index("row"), lax.axis_index("col")
    field = ext_ref[...].astype(jnp.float32)
    first, second = taps_of(weight_refs, 0), taps_of(weight_refs, 1)
    hidden = jnp.dot(first, tap_stack(field, pitch, 0), preferred_element_type=jnp.float32)
    hidden = jnp.maximum(hidden + bias_ref[0], 0.0)
    pixel = lax.broadcasted_iota(jnp.int32, (1, total), 1) + 1
    y = lax.shift_right_logical(pixel, pitch.bit_length() - 1)
    x = pixel & (pitch - 1)
    top = jnp.where(place == 0, 1, -1)
    bottom = jnp.where(place == lax.axis_size("row") - 1, tile_rows + 2, -1)
    left = jnp.where(col == 0, 0, -1)
    right = jnp.where(col == lax.axis_size("col") - 1, tile_cols + 1, -1)
    inside = (y != top) & (y != bottom) & (x != left) & (x != right)
    hidden = jnp.where(inside, hidden, 0.0).astype(jnp.bfloat16).astype(jnp.float32)
    narrow = tile_cols == LANES
    rows_kept = tile_rows if narrow else 0
    after = jnp.dot(
        second, tap_stack(hidden, pitch, rows_kept), preferred_element_type=jnp.float32
    )
    if narrow:
        field = jnp.concatenate(
            [field[:, y * pitch : y * pitch + LANES] for y in range(2, tile_rows + 2)], axis=1
        )
    settled = jnp.maximum(after + bias_ref[1] + field, 0.0)
    strip_rows = tile_rows // STRIPS
    lane = lax.broadcasted_iota(jnp.int32, (1, LANES), 1)
    for strip in range(STRIPS):
        groups = []
        if narrow:
            groups = [
                settled[:, y * LANES : (y + 1) * LANES]
                for y in range(strip * strip_rows, (strip + 1) * strip_rows)
            ]
        else:
            per_group = min(LANES // tile_cols, strip_rows)
            for start in range(0, strip_rows, per_group):
                merged = None
                for turn in range(per_group):
                    at = (strip * strip_rows + start + turn + 2) * pitch
                    part = settled[:, at // LANES * LANES : at // LANES * LANES + LANES]
                    shift = (turn * tile_cols - at) % LANES
                    part = pltpu.roll(part, shift, 1) if shift else part
                    merged = part if turn == 0 else jnp.where(lane < turn * tile_cols, merged, part)
                groups.append(merged)
        if len(groups) == 1:
            groups = folded(groups[0], strip_rows * tile_cols)
        size = groups[0].shape[0]
        for at, group in enumerate(groups):
            strips_ref[strip, at * size : (at + 1) * size] = group.astype(jnp.bfloat16)


def deep_block(branch_level, tiles, kernels, biases):
    channels = WIDTH << branch_level
    extended = tiles[branch_level]
    if channels == kernels.shape[-1] and channels % LANES == 0:
        weights = [kernels]
    else:
        weights = [
            jnp.concatenate(
                [
                    kernels[layer, dy, dx, :channels, :channels]
                    for dy in range(3)
                    for dx in range(3)
                ],
                axis=1,
            )
            for layer in range(2)
        ]
    vmem = pl.BlockSpec(memory_space=pltpu.VMEM)
    return pl.pallas_call(
        partial(block_kernel, branch_level),
        out_shape=jax.ShapeDtypeStruct((STRIPS, PIECE_ROWS, LANES), jnp.bfloat16),
        in_specs=[vmem] * (2 + len(weights)),
        out_specs=vmem,
        compiler_params=pltpu.CompilerParams(vmem_limit_bytes=60 << 20),
        name=f"block_{branch_level}",
    )(extended, biases[:, :channels, None], *weights)


LANES = 128
STRIPS = 4
PIECE_ROWS = WIDTH * TH * TW // (STRIPS * LANES)
MESH = pl.DeviceIdType.MESH


def piece_rows(branch_level):
    return PIECE_ROWS >> branch_level


def block_mask(fine_level, coarse_level):
    fine_cols = TW >> fine_level
    coarse_cols = TW >> coarse_level
    fine = TH * TW // STRIPS >> 2 * fine_level
    coarse = TH * TW // STRIPS >> 2 * coarse_level
    shift = coarse_level - fine_level
    pixel = lax.broadcasted_iota(jnp.int32, (fine, 1), 0)
    row = lax.shift_right_logical(pixel, fine_cols.bit_length() - 1 + shift)
    col = lax.shift_right_logical(pixel & (fine_cols - 1), shift)
    home = row * coarse_cols + col
    target = lax.broadcasted_iota(jnp.int32, (fine, coarse), 1)
    return jnp.where(home == target, 1.0, 0.0).astype(jnp.bfloat16)


def mixed(weight_ref, target, source, tile_data):
    start = ((1 << source) - 1) * WIDTH
    low = start // LANES * LANES
    high = min(-(-(start + tile_data.shape[0]) // LANES) * LANES, weight_ref.shape[1])
    pieces = []
    if start > low:
        pieces.append(jnp.zeros((start - low, tile_data.shape[1]), tile_data.dtype))
    pieces.append(tile_data)
    if high > start + tile_data.shape[0]:
        pieces.append(
            jnp.zeros((high - start - tile_data.shape[0], tile_data.shape[1]), tile_data.dtype)
        )
    rows = ((1 << target) - 1) * WIDTH
    return jnp.dot(
        weight_ref[rows : rows + (WIDTH << target), low:high],
        jnp.concatenate(pieces, axis=0),
        preferred_element_type=jnp.float32,
    ).astype(jnp.bfloat16)


def join_strip(maps, masks, weight_ref, bias_ref, out_refs):
    for target in range(4):
        start = ((1 << target) - 1) * WIDTH
        total = maps[target].astype(jnp.float32) + bias_ref[start : start + (WIDTH << target), :]
        for source in range(4):
            if source < target:
                share = 0.25 ** (target - source)
                shrunk = jnp.dot(
                    maps[source], masks[source, target], preferred_element_type=jnp.float32
                )
                term = mixed(weight_ref, target, source, (shrunk * share).astype(jnp.bfloat16))
                total = total + term.astype(jnp.float32)
            elif source > target:
                term = mixed(weight_ref, target, source, maps[source])
                total = total + lax.dot_general(
                    term,
                    masks[target, source],
                    (((1,), (1,)), ((), ())),
                    preferred_element_type=jnp.float32,
                )
        total = jnp.maximum(total, 0.0)
        out_ref = out_refs[target]
        if len(out_ref.shape) == 2:
            out_ref[...] = total.T.astype(jnp.bfloat16)
        else:
            lines = [total[:, at : at + LANES] for at in range(0, total.shape[1], LANES)]
            out_ref[...] = jnp.stack(lines, axis=1).astype(jnp.bfloat16)


def exchange_kernel(
    strips_ref, held, relay, near_send, near_recv, far_send, far_recv, own_sem
):
    level = lax.axis_index("branch")
    place = lax.axis_index("row")
    col = lax.axis_index("col")
    size = STRIPS
    home = level == place

    barrier = pltpu.get_barrier_semaphore()
    for step in range(1, size):
        for device in (
            (level, lax.rem(place + step, size), col),
            (lax.rem(level + step, size), place, col),
        ):
            pl.semaphore_signal(barrier, inc=1, device_id=device, device_id_type=MESH)
    pl.semaphore_wait(barrier, 2 * (size - 1))

    def near(rows, step):
        strip = lax.rem(place + step, size)
        return pltpu.make_async_remote_copy(
            src_ref=strips_ref.at[strip, 0:rows],
            dst_ref=relay.at[step - 1, 0:rows],
            send_sem=near_send.at[step - 1],
            recv_sem=near_recv.at[step - 1],
            device_id=(level, strip, col),
            device_id_type=MESH,
        )

    def far(source, step):
        rows = piece_rows(source)
        tile = lax.rem(place + size - step, size)
        piece = strips_ref.at[place, 0:rows] if step == 0 else relay.at[step - 1, 0:rows]
        return (
            tile,
            pltpu.make_async_remote_copy(
                src_ref=piece,
                dst_ref=held.at[source, 0:rows],
                send_sem=far_send.at[step],
                recv_sem=far_recv.at[source],
                device_id=(tile, place, col),
                device_id_type=MESH,
            ),
            pltpu.make_async_copy(piece, held.at[source, 0:rows], own_sem),
        )

    def onward(source):
        rows = piece_rows(source)
        for step in (2, 1, 3):
            near(rows, step).start()
        for step in (0, 1, 3, 2):
            if step:
                near(rows, step).wait_recv()
            tile, remote, own = far(source, step)
            pl.when(tile != level)(remote.start)
            pl.when(tile == level)(own.start)

    for source in range(size):
        pl.when(level == source)(partial(onward, source))

    for source in range(size):
        _, remote, own = far(source, 0)
        pl.when(level != source)(remote.wait_recv)
        pl.when(level == source)(own.wait)

    def sent(source):
        for step in range(1, size):
            near(piece_rows(source), step).wait_send()
        for step in range(size):
            tile, remote, _ = far(source, step)
            pl.when(tile != level)(remote.wait_send)

    for source in range(size):
        pl.when(level == source)(partial(sent, source))


def join_kernel(held, weight_ref, bias_ref, *out_refs):
    masks = {
        (fine, coarse): block_mask(fine, coarse)
        for fine in range(3)
        for coarse in range(fine + 1, 4)
    }
    maps = []
    for source in range(4):
        channels = WIDTH << source
        pixels = TH * TW // STRIPS >> 2 * source
        if pixels >= LANES:
            maps.append(
                jnp.concatenate(
                    [
                        held[source, at * channels : (at + 1) * channels]
                        for at in range(pixels // LANES)
                    ],
                    axis=1,
                )
            )
        else:
            piece = held[source, 0 : piece_rows(source)].astype(jnp.float32)
            unfolded = jnp.concatenate(
                [turned(piece, -turn * pixels) for turn in range(LANES // pixels)], axis=0
            )
            maps.append(unfolded.astype(jnp.bfloat16)[:, :pixels])
    join_strip(maps, masks, weight_ref, bias_ref, out_refs)


def joined(strips, join_weight, join_bias):
    vmem = pl.BlockSpec(memory_space=pltpu.VMEM)
    held = pl.pallas_call(
        exchange_kernel,
        out_shape=jax.ShapeDtypeStruct((STRIPS, PIECE_ROWS, LANES), jnp.bfloat16),
        in_specs=[vmem],
        out_specs=vmem,
        scratch_shapes=[
            pltpu.VMEM((STRIPS - 1, PIECE_ROWS, LANES), jnp.bfloat16),
            pltpu.SemaphoreType.DMA((STRIPS - 1,)),
            pltpu.SemaphoreType.DMA((STRIPS - 1,)),
            pltpu.SemaphoreType.DMA((STRIPS,)),
            pltpu.SemaphoreType.DMA((STRIPS,)),
            pltpu.SemaphoreType.DMA,
        ],
        compiler_params=pltpu.CompilerParams(collective_id=0, has_side_effects=True),
        name="exchange",
    )(strips)
    shapes = [(WIDTH << b, (TH >> b) // STRIPS, TW >> b) for b in range(4)]
    outs = pl.pallas_call(
        join_kernel,
        out_shape=[
            jax.ShapeDtypeStruct(
                shape if shape[2] == LANES else (shape[1] * shape[2], shape[0]), jnp.bfloat16
            )
            for shape in shapes
        ],
        in_specs=[vmem] * 3,
        out_specs=[vmem] * 4,
        name="join",
    )(held, join_weight, join_bias[:, None])
    return tuple(
        out if out.ndim == 3 else out.reshape(*shape[1:], shape[0]).transpose(2, 0, 1)
        for out, shape in zip(outs, shapes)
    )


def local(section_in, conv_weight, conv_bias, join_weight, join_bias):
    level_index = lax.axis_index("branch")
    container = section_in[0, 0, 0]
    kernels = conv_weight[0]
    biases = conv_bias[0]
    tiles = extended_tiles(container)
    strips = lax.switch(
        level_index,
        [partial(deep_block, branch_level) for branch_level in range(4)],
        tiles,
        kernels,
        biases,
    )
    return tuple(joined(strips, join_weight, join_bias))


def solution(mesh):
    in_specs = (
        P("branch", "row", "col", None, None),
        P("branch", None, None, None, None, None),
        P("branch", None, None),
        P(),
        P(),
    )
    out_specs = (
        P(None, ("branch", "row"), "col"),
        P(None, ("branch", "row"), "col"),
        P(None, ("branch", "row"), "col"),
        P(None, ("branch", "row"), "col"),
    )
    return jax.shard_map(local, mesh=mesh, in_specs=in_specs, out_specs=out_specs, check_vma=False)
```

profile of v0, /device:TPU:0, one launch (start us, length us, event | category | flops | bytes accessed | tf_op | source)
XLA Modules:
  0.0 41.9 jit_solution(17484092342283918625)
XLA Ops:
  0.6 8.5 %halo.1 = (bf16[48,9216]{1,0:T(8,128)(2,1)S(1)}, bf16[96,2560]{1,0:T(8,128)(2,1)S(1)}, bf16[192,768]{1,0:T(8,128)(2,1)S(1)}, bf16[384,256]{1,0:T(8,128)(2,1)S(1)}) custom-call(bf16[48,4096]{1,0:T(8,128)(2,1)} %bitcast.131), custom_call_target="tpu_custom_call" | custom-call | tf_op jit(solution)/shard_map/halo/pallas_call | solution.py:183
  9.1 0.0 copy-start.1
  9.2 6.8 %conditional.1 = (bf16[4,384,128]{2,1,0:T(8,128)(2,1)S(1)}) conditional(s32[]{:T(128)} %clamp.3, (f32[2,384]{1,0:T(2,128)}, bf16[2,3,3,384,384]{4,3,2,1,0:T(8,128)(2,1)}, bf16[48,9216]{1,0:T(8,128)(2,1)S(1)}) %tuple.84, (f32[2,384]{1,0:T(2,128)}, bf16[2,3,3,384,384]{4,3,2,1,0:T(8,128)(2,1)}, ...), branch_computations={%region_0.0_spmd, %region_1.0_spmd, %region_2.0_spmd, %region_3.0_... | conditional | bytes 5326884 | solution.py:557
  9.2 0.9 %slice_bitcast_fusion = (bf16[48,48]{1,0:T(8,128)(2,1)S(1)}, bf16[48,48]{1,0:T(8,128)(2,1)S(1)}, bf16[48,48]{1,0:T(8,128)(2,1)S(1)}, bf16[48,48]{1,0:T(8,128)(2,...) fusion(bf16[2,3,3,384,384]{4,3,2,1,0:T(8,128)(2,1)} %get-tuple-, ...), kind=kLoop, calls=%fused_computation | loop fusion | bytes 165888 | tf_op jit(solution)/shard_map/cond/branch_0_fun/squeeze | solution.py:317
  10.1 0.7 %concatenate.13.refs_1_ = bf16[48,432]{1,0:T(8,128)(2,1)} concatenate(bf16[48,48]{1,0:T(8,128)(2,1)S(1)} %get-tuple-element.69, bf16[48,48]{1,0:T(8,128)(2,1)S(1)} %get-tuple-element.68, bf16[48,48]{1,0:T(8,128)(2,1)S(1)} %get-tuple-element.67, bf16[48,48]{1,0:T(8,128)(2,1)S(1)} %get-tuple-element.66, bf16[48,48]{1,0:T(8,128)(2,1)S(1)} %get-tuple-element.65, ...), dimensions={1} | concatenate | bytes 82944 | tf_op jit(solution)/shard_map/cond/branch_0_fun/concatenate | solution.py:315
  10.8 0.7 %concatenate.12.refs_0_ = bf16[48,432]{1,0:T(8,128)(2,1)} concatenate(bf16[48,48]{1,0:T(8,128)(2,1)S(1)} %get-tuple-element.78, bf16[48,48]{1,0:T(8,128)(2,1)S(1)} %get-tuple-element.77, bf16[48,48]{1,0:T(8,128)(2,1)S(1)} %get-tuple-element.76, bf16[48,48]{1,0:T(8,128)(2,1)S(1)} %get-tuple-element.75, bf16[48,48]{1,0:T(8,128)(2,1)S(1)} %get-tuple-element.74, ...), dimensions={1} | concatenate | bytes 82944 | tf_op jit(solution)/shard_map/cond/branch_0_fun/concatenate | solution.py:315
  11.6 0.7 %slice_bitcast_fusion.18 = f32[2,48,1]{1,0,2:T(2,128)S(1)} fusion(f32[2,384]{1,0:T(2,128)} %get-tuple-element.26), kind=kLoop, calls=%fused_computation.18 | loop fusion | bytes 768 | tf_op jit(solution)/shard_map/cond/branch_0_fun/broadcast_in_dim | solution.py:333
  12.2 0.7 %copy.10.bias_ref = f32[2,48,1]{2,1,0:T(8,128)} copy(f32[2,48,1]{1,0,2:T(2,128)S(1)} %slice_bitcast_fusion.18) | data formatting | bytes 768 | tf_op jit(solution)/shard_map/cond/branch_0_fun/broadcast_in_dim | solution.py:333
  13.0 3.0 %block_0.1 = bf16[4,384,128]{2,1,0:T(8,128)(2,1)S(1)} custom-call(bf16[48,9216]{1,0:T(8,128)(2,1)S(1)} %get-tuple-element.25.ext_ref, f32[2,48,1]{2,1,0:T(8,128)} %copy.10.bias_ref, bf16[48,432]{1,0:T(8,128)(2,1)} %concatenate.12.refs_0_, bf16[48,432]{1,0:T(8,128)(2,1)} %concatenate.13.refs_1_), custom_call_target="tpu_custom_call" | custom-call | tf_op jit(solution)/shard_map/cond/branch_0_fun/block_0/pallas_call | solution.py:326
  16.0 20.7 %exchange.1.held = bf16[4,384,128]{2,1,0:T(8,128)(2,1)} custom-call(bf16[4,384,128]{2,1,0:T(8,128)(2,1)S(1)} %get-tuple-element.115.strips_ref), custom_call_target="tpu_custom_call" | custom-call | tf_op jit(solution)/shard_map/exchange/pallas_call | solution.py:516
  36.7 0.0 copy-done.1
  36.7 0.9 %broadcast_in_dim.13.bias_ref = f32[720,1]{1,0:T(8,128)} reshape(f32[720]{0:T(1024)S(1)} %copy-done.1) | data formatting | bytes 5760 | tf_op jit(solution)/shard_map/broadcast_in_dim | solution.py:544
  37.6 4.3 %join.1 = (bf16[48,8,128]{2,1,0:T(8,128)(2,1)}, bf16[256,96]{1,0:T(8,128)(2,1)}, bf16[64,192]{1,0:T(8,128)(2,1)}, bf16[16,384]{1,0:T(8,128)(2,1)}) custom-call(bf16[4,384,128]{2,1,0:T(8,128)(2,1)} %exchange.1.held, bf16[720,720]{1,0:T(8,128)(2,1)} %weight_ref.1, f32[720,1]{1,0:T(8,128)} %broadcast_in_dim.13.bias_ref), custom_call_target="tpu_custom_call" | custom-call | tf_op jit(solution)/shard_map/join/pallas_call | solution.py:533
Async XLA Ops:
  9.1 27.5 %copy-start.1 = (f32[720]{0:T(1024)S(1)}, f32[720]{0:T(1024)}, u32[]{:S(2)}) copy-start(f32[720]{0:T(1024)} %param.13) | copy-start | bytes 8644
where the time goes:
time: 42.2 us; the launch traced here: 41.9 us
  Pallas kernels  36.5 us (86%)
  local copies, waits for them, and re-layouts  4.69 us (11%)
  between operations  0.68 us (2%)
    pallas_call x1, Pallas kernels, joined(): pl.pallas_call(exchange_kernel, out_shape=jax.ShapeDtypeStruct((STRIPS, P...  20.7 us
    pallas_call x1, Pallas kernels, extended_tiles(): pl.pallas_call(halo_kernel, out_shape=[jax.ShapeDtypeStruct((WIDTH << b,...  8.51 us
    pallas_call x1, Pallas kernels, joined(): pl.pallas_call(join_kernel, out_shape=[jax.ShapeDtypeStruct(shape if shap...  4.27 us
    pallas_call x1, Pallas kernels, deep_block(): pl.pallas_call(partial(block_kernel, branch_level), out_shape=jax.ShapeDt...  3 us
    concatenate x2, local copies, waits for them, and re-layouts, deep_block(): jnp.concatenate([kernels[layer, dy, dx, :channels, :channels] for dy in r...  1.47 us
    broadcast_in_dim x2, local copies, waits for them, and re-layouts, deep_block(): biases[:, :channels, None]  1.4 us
    squeeze x1, local copies, waits for them, and re-layouts, deep_block(): kernels[layer, dy, dx, :channels, :channels]  0.91 us
    broadcast_in_dim x1, local copies, waits for them, and re-layouts, joined(): join_bias[:, None]  0.89 us

commit v1 on v0

v1 whole, which is shorter than its diff:
```python
from functools import partial

import jax
import jax.numpy as jnp
from jax import lax
from jax.experimental import pallas as pl
from jax.experimental.pallas import tpu as pltpu
from jax.sharding import PartitionSpec as P

WIDTH = 48
TH = 32
TW = 128
LANES = 128
STRIPS = 4
MESH = pl.DeviceIdType.MESH
WAYS = [(dr, dc) for dr in (-1, 0, 1) for dc in (-1, 0, 1) if dr or dc]
F32 = jnp.float32
BF16 = jnp.bfloat16

OWN_TILES = (32, 8, 2, 1)
BEFORE = (2, 1, 1, 0)
FIELD_TILES = (36, 10, 4, 1)
HIDDEN_TILES = (34, 10, 4, 1)


def lane_index(width=LANES):
    return lax.broadcasted_iota(jnp.int32, (1, width), 1)


def turned(group, shift):
    shift = shift % LANES
    return pltpu.roll(group, shift, 1) if shift else group


def tiles_turned(field, shift):
    if shift % LANES == 0:
        return field
    tiles = [turned(field[:, t : t + LANES], shift) for t in range(0, field.shape[1], LANES)]
    return tiles[0] if len(tiles) == 1 else jnp.concatenate(tiles, axis=1)


def natural_tile(branch_level, container_ref):
    pixels = TH * TW >> 2 * branch_level
    channels = WIDTH << branch_level
    parts = []
    for part in range(1 << branch_level):
        at = part * pixels
        low = at // LANES * LANES
        piece = container_ref[:, low : low + max(pixels, LANES)]
        if at > low:
            piece = pltpu.roll(piece.astype(F32), LANES - at + low, 1).astype(BF16)
        parts.append(piece)
    held = lax.broadcasted_iota(jnp.int32, (1, channels), 1)
    part = sum((held >= WIDTH * turn).astype(jnp.int32) for turn in range(1, 1 << branch_level))
    home = ((held - WIDTH * part) << branch_level) + part
    order = jnp.where(lax.broadcasted_iota(jnp.int32, (channels, channels), 0) == home, 1.0, 0.0)
    return jnp.dot(
        order.astype(BF16), jnp.concatenate(parts, axis=0), preferred_element_type=F32
    ).astype(BF16)


def column_stack(branch_level, own, west, east):
    cols = TW >> branch_level
    col = lane_index(own.shape[1]) & (cols - 1)
    own32 = own.astype(F32)
    minus = tiles_turned(
        jnp.where(col == cols - 1, tiles_turned(west.astype(F32), -cols), own32), 1
    ).astype(BF16)
    plus = tiles_turned(
        jnp.where(col == 0, tiles_turned(east.astype(F32), cols), own32), -1
    ).astype(BF16)

    def zeros(rows):
        return jnp.zeros((rows, own.shape[1]), BF16)

    if branch_level == 0:
        pieces = [minus, own, zeros(32), plus, zeros(80)]
    elif branch_level == 3:
        pieces = [minus, own, plus]
    else:
        pad = zeros(-own.shape[0] % LANES)
        pieces = [minus, pad, own, pad, plus, pad]
    return jnp.concatenate(pieces, axis=0)


def taps(branch_level, weights, layer):
    channels = WIDTH << branch_level
    width = -(-channels // LANES) * LANES
    lines = []
    for dy in range(3):
        if branch_level == 0:
            first, middle, last = (weights[layer, dy, dx, 0:channels, 0:width] for dx in range(3))
            pair = jnp.where(
                lane_index() < channels,
                first.astype(F32),
                pltpu.roll(middle.astype(F32), channels, 1),
            )
            lines.append(jnp.concatenate([pair.astype(BF16), last], axis=1))
        else:
            lines.append(
                jnp.concatenate(
                    [weights[layer, dy, dx, 0:channels, 0:width] for dx in range(3)], axis=1
                )
            )
    return jnp.concatenate(lines, axis=0)


def row_sum(branch_level, products, first, count):
    channels = products.shape[0] // 3
    cols = TW >> branch_level
    above, here, below = (products[d * channels : (d + 1) * channels] for d in range(3))
    span = slice(first * LANES, (first + count) * LANES)
    if cols == LANES:
        return (
            above[:, (first - 1) * LANES : (first - 1 + count) * LANES]
            + here[:, span]
            + below[:, (first + 1) * LANES : (first + 1 + count) * LANES]
        )
    last = products.shape[1] // LANES - 1
    above, below = tiles_turned(above, cols), tiles_turned(below, -cols)
    lane = lane_index()

    def tile(field, t):
        t = min(max(t, 0), last)
        return field[:, t * LANES : (t + 1) * LANES]

    tiles = [
        jnp.where(lane < cols, tile(above, t - 1), tile(above, t))
        + tile(here, t)
        + jnp.where(lane >= LANES - cols, tile(below, t + 1), tile(below, t))
        for t in range(first, first + count)
    ]
    return tiles[0] if count == 1 else jnp.concatenate(tiles, axis=1)


def front_kernel(
    section, kernels, biases, held0, held1, held2, held3,
    container, weights, bias, own0, own1, own2, own3, side0, side1, side2, side3,
    pack_send, pack_recv, hide0, hide1, hide2, hide3, hid0, hid1, hid2, hid3,
    settled0, settled1, settled2, settled3, load_sem,
    halo_send, halo_recv, hidden_send, hidden_recv, strip_send, strip_recv, own_sem,
):
    level = lax.axis_index("branch")
    place = lax.axis_index("row")
    col = lax.axis_index("col")
    row_count = lax.axis_size("row")
    col_count = lax.axis_size("col")

    def reach(dr, dc):
        there = jnp.bool_(True)
        if dr:
            there = (place + dr >= 0) & (place + dr < row_count)
        if dc:
            sideways = (col + dc >= 0) & (col + dc < col_count)
            there = there & sideways if dr else sideways
        device = (
            level,
            lax.rem(place + dr + row_count, row_count),
            lax.rem(col + dc + col_count, col_count),
        )
        return there, device

    barrier = pltpu.get_barrier_semaphore()
    expected = 0
    for dr, dc in WAYS:
        there, device = reach(dr, dc)
        expected = expected + there.astype(jnp.int32)

        @pl.when(there)
        def _():
            pl.semaphore_signal(barrier, inc=1, device_id=device, device_id_type=MESH)

    at_home = level == place
    for source in range(STRIPS):

        @pl.when(jnp.logical_not(at_home & (level == source)))
        def _():
            pl.semaphore_signal(
                barrier, inc=1, device_id=(source, level, col), device_id_type=MESH
            )

    expected = expected + STRIPS - at_home.astype(jnp.int32)

    helds = (held0, held1, held2, held3)
    owns = (own0, own1, own2, own3)
    sides = (side0, side1, side2, side3)
    hides = (hide0, hide1, hide2, hide3)
    hids = (hid0, hid1, hid2, hid3)
    settleds = (settled0, settled1, settled2, settled3)

    def run(b):
        channels = WIDTH << b
        width = -(-channels // LANES) * LANES
        cols, rows = TW >> b, TH >> b
        own, side, hide, hid = owns[b], sides[b], hides[b], hids[b]
        settled, held = settleds[b], helds[b]
        before, tiles = BEFORE[b], OWN_TILES[b]
        middle = slice(before * LANES, (before + tiles) * LANES)

        if b == 0:
            load = pltpu.make_async_copy(section, own.at[:, middle], load_sem.at[0])
        else:
            load = pltpu.make_async_copy(
                section.at[:, 0 : TH * TW >> b], container.at[:, 0 : TH * TW >> b], load_sem.at[0]
            )
        load.start()
        bias_load = pltpu.make_async_copy(biases, bias, load_sem.at[1])
        bias_load.start()
        weight_loads = [
            pltpu.make_async_copy(
                kernels.at[layer, :, :, 0:channels, 0:width],
                weights.at[layer, :, :, 0:channels, 0:width],
                load_sem.at[2 + layer],
            )
            for layer in range(2)
        ]
        for copy in weight_loads:
            copy.start()
        load.wait()
        if b:
            own[:, middle] = natural_tile(b, container)
        packed = b == 3
        lane = lane_index()
        if packed:
            whole = own[...].astype(F32)
            for end in range(2):
                out = None
                for g in range(4):
                    part = turned(whole[g * 96 : (g + 1) * 96], 32 * g - 32 * end)
                    out = part if g == 0 else jnp.where(lane < 32 * g, out, part)
                pack_send[end] = out.astype(BF16)

        def halo_region(dr, dc):
            if packed and dr:
                return pack_recv.at[WAYS.index((dr, dc))]
            target = own if dc == 0 else side.at[0 if dc == 1 else 1]
            if dr == 0:
                return target.at[:, middle]
            if dr == 1:
                return target.at[:, 0 : before * LANES]
            return target.at[:, (before + tiles) * LANES : (before + tiles + before) * LANES]

        def halo_source(dr):
            if dr == 0:
                return own.at[:, middle]
            if packed:
                return pack_send.at[0 if dr == -1 else 1]
            first = before if dr == -1 else tiles
            return own.at[:, first * LANES : (first + before) * LANES]

        def halo_copy(dr, dc):
            way = WAYS.index((dr, dc))
            return pltpu.make_async_remote_copy(
                src_ref=halo_source(dr),
                dst_ref=halo_region(dr, dc),
                send_sem=halo_send.at[way],
                recv_sem=halo_recv.at[way],
                device_id=reach(dr, dc)[1],
                device_id_type=MESH,
            )

        order = [way for way in WAYS if way[0]] + [way for way in WAYS if not way[0]]
        pl.semaphore_wait(barrier, expected)
        for dr, dc in order:
            pl.when(reach(dr, dc)[0])(halo_copy(dr, dc).start)
        for dr, dc in order:

            @pl.when(jnp.logical_not(reach(-dr, -dc)[0]))
            def _():
                region = halo_region(dr, dc)
                region[...] = jnp.zeros(region.shape, BF16)

        bias_load.wait()
        offsets = [
            jnp.broadcast_to(bias[layer : layer + 1, :], (8, bias.shape[1])).T[:channels, 0:1]
            for layer in range(2)
        ]
        weight_loads[0].wait()
        for dr, dc in order:
            pl.when(reach(-dr, -dc)[0])(halo_copy(dr, dc).wait_recv)

        fields = [own[...], side[0], side[1]]
        if packed:
            for at, dc in enumerate((0, 1, -1)):
                upper = pack_recv[WAYS.index((1, dc))].astype(F32)
                lower = pack_recv[WAYS.index((-1, dc))].astype(F32)
                lines = []
                for g in range(4):
                    here = fields[at][g * 96 : (g + 1) * 96].astype(F32)
                    ring = jnp.where(
                        lane < 96, turned(lower, 64 - 32 * g), turned(upper, 96 - 32 * g)
                    )
                    lines.append(jnp.where(lane < 64, here, ring).astype(BF16))
                fields[at] = jnp.concatenate(lines, axis=0)

        products = jnp.dot(
            taps(b, weights, 0),
            column_stack(b, *fields),
            preferred_element_type=F32,
        )
        first = 1 if b == 0 else 0
        hidden = row_sum(b, products, first, HIDDEN_TILES[b])
        hidden = jnp.maximum(hidden + offsets[0], 0.0)
        row = lax.shift_right_logical(lane_index(HIDDEN_TILES[b] * LANES), cols.bit_length() - 1)
        if b == 3:
            row = jnp.where(row >= 6, row - 8, row)
        else:
            row = row - (before - first) * (LANES // cols)
        low = jnp.where(place == 0, 0, -LANES)
        high = jnp.where(place == row_count - 1, rows, 2 * LANES)
        hidden = jnp.where((row >= low) & (row < high), hidden, 0.0)
        hid[...] = hidden.astype(BF16)

        def hidden_copy(dc):
            at = 0 if dc == 1 else 1
            return pltpu.make_async_remote_copy(
                src_ref=hid,
                dst_ref=hide.at[at],
                send_sem=hidden_send.at[at],
                recv_sem=hidden_recv.at[at],
                device_id=reach(0, dc)[1],
                device_id_type=MESH,
            )

        for dc in (1, -1):
            pl.when(reach(0, dc)[0])(hidden_copy(dc).start)
        for dc in (1, -1):

            @pl.when(jnp.logical_not(reach(0, -dc)[0]))
            def _():
                at = 0 if dc == 1 else 1
                hide[at] = jnp.zeros(hid.shape, BF16)

        weight_loads[1].wait()
        for dc in (1, -1):
            pl.when(reach(0, -dc)[0])(hidden_copy(dc).wait_recv)
        products = jnp.dot(
            taps(b, weights, 1),
            column_stack(b, hid[...], hide[0], hide[1]),
            preferred_element_type=F32,
        )
        after = row_sum(b, products, 1 if b == 0 else before, tiles)
        final = jnp.maximum(after + offsets[1] + own[:, middle].astype(F32), 0.0)
        if b < 3:
            settled[...] = final.astype(BF16)
        else:
            for strip in range(STRIPS):
                out = None
                for g in range(8):
                    part = turned(final[g * WIDTH : (g + 1) * WIDTH], 16 * g - 16 * strip)
                    out = part if g == 0 else jnp.where(lane < 16 * g, out, part)
                settled[strip] = out.astype(BF16)

        def strip_source(strip):
            if b == 3:
                return settled.at[strip]
            if b == 2:
                return settled.at[:, pl.ds(pl.multiple_of(strip // 2 * LANES, LANES), LANES)]
            size = tiles * LANES // STRIPS
            return settled.at[:, pl.ds(pl.multiple_of(strip * size, LANES), size)]

        def strip_copies(turn):
            strip = lax.rem(place + turn, STRIPS)
            source = strip_source(strip)
            remote = pltpu.make_async_remote_copy(
                src_ref=source,
                dst_ref=held,
                send_sem=strip_send.at[turn],
                recv_sem=strip_recv.at[b],
                device_id=(place, strip, col),
                device_id_type=MESH,
            )
            return remote, pltpu.make_async_copy(source, held, own_sem)

        for turn in range(STRIPS):
            remote, local_copy = strip_copies(turn)
            if turn == 0:
                pl.when(jnp.logical_not(at_home))(remote.start)
                pl.when(at_home)(local_copy.start)
            else:
                remote.start()

        for dr, dc in order:
            pl.when(reach(dr, dc)[0])(halo_copy(dr, dc).wait_send)
        for dc in (1, -1):
            pl.when(reach(0, dc)[0])(hidden_copy(dc).wait_send)
        for turn in range(STRIPS):
            remote, local_copy = strip_copies(turn)
            if turn == 0:
                pl.when(jnp.logical_not(at_home))(remote.wait_send)
                pl.when(at_home)(local_copy.wait)
            else:
                remote.wait_send()

    for b in range(STRIPS):
        pl.when(level == b)(partial(run, b))

    for source in range(STRIPS):
        arrival = pltpu.make_async_remote_copy(
            src_ref=helds[source],
            dst_ref=helds[source],
            send_sem=strip_send.at[0],
            recv_sem=strip_recv.at[source],
            device_id=(source, level, col),
            device_id_type=MESH,
        )
        pl.when(jnp.logical_not(at_home & (level == source)))(arrival.wait_recv)


HELD_SHAPES = ((48, 1024), (96, 256), (192, 128), (48, 128))


def front(section, kernels, biases):
    anywhere = pl.BlockSpec(memory_space=pl.ANY)
    vmem = pl.BlockSpec(memory_space=pltpu.VMEM)

    def field(b, tiles):
        return (WIDTH << b, tiles[b] * LANES)

    scratch = [
        pltpu.VMEM((WIDTH, TH * TW // 2), BF16),
        pltpu.VMEM(kernels.shape, BF16),
        pltpu.VMEM(biases.shape, F32),
    ]
    scratch += [pltpu.VMEM(field(b, FIELD_TILES), BF16) for b in range(4)]
    scratch += [pltpu.VMEM((2, *field(b, FIELD_TILES)), BF16) for b in range(4)]
    scratch += [pltpu.VMEM((2, 96, LANES), BF16), pltpu.VMEM((8, 96, LANES), BF16)]
    scratch += [pltpu.VMEM((2, *field(b, HIDDEN_TILES)), BF16) for b in range(4)]
    scratch += [pltpu.VMEM(field(b, HIDDEN_TILES), BF16) for b in range(4)]
    scratch += [pltpu.VMEM(field(b, OWN_TILES), BF16) for b in range(3)]
    scratch += [pltpu.VMEM((STRIPS, WIDTH, LANES), BF16)]
    dma = pltpu.SemaphoreType.DMA
    scratch += [dma((4,)), dma((8,)), dma((8,)), dma((2,)), dma((2,)), dma((4,)), dma((4,)), dma]
    return pl.pallas_call(
        front_kernel,
        out_shape=[jax.ShapeDtypeStruct(shape, BF16) for shape in HELD_SHAPES],
        in_specs=[anywhere] * 3,
        out_specs=[vmem] * 4,
        scratch_shapes=scratch,
        compiler_params=pltpu.CompilerParams(
            collective_id=0, has_side_effects=True, vmem_limit_bytes=56 << 20
        ),
        name="front",
    )(section, kernels, biases)


def block_mask(fine_level, coarse_level):
    fine_cols = TW >> fine_level
    coarse_cols = TW >> coarse_level
    fine = TH * TW // STRIPS >> 2 * fine_level
    coarse = TH * TW // STRIPS >> 2 * coarse_level
    shift = coarse_level - fine_level
    pixel = lax.broadcasted_iota(jnp.int32, (fine, 1), 0)
    row = lax.shift_right_logical(pixel, fine_cols.bit_length() - 1 + shift)
    col = lax.shift_right_logical(pixel & (fine_cols - 1), shift)
    home = row * coarse_cols + col
    target = lax.broadcasted_iota(jnp.int32, (fine, coarse), 1)
    return jnp.where(home == target, 1.0, 0.0).astype(BF16)


def mixed(weight_ref, target, source, tile_data):
    start = ((1 << source) - 1) * WIDTH
    low = start // LANES * LANES
    high = min(-(-(start + tile_data.shape[0]) // LANES) * LANES, weight_ref.shape[1])
    pieces = []
    if start > low:
        pieces.append(jnp.zeros((start - low, tile_data.shape[1]), tile_data.dtype))
    pieces.append(tile_data)
    if high > start + tile_data.shape[0]:
        pieces.append(
            jnp.zeros((high - start - tile_data.shape[0], tile_data.shape[1]), tile_data.dtype)
        )
    rows = ((1 << target) - 1) * WIDTH
    return jnp.dot(
        weight_ref[rows : rows + (WIDTH << target), low:high],
        jnp.concatenate(pieces, axis=0),
        preferred_element_type=F32,
    ).astype(BF16)


def join_strip(maps, masks, weight_ref, offset, out_refs):
    for target in range(4):
        start = ((1 << target) - 1) * WIDTH
        total = maps[target].astype(F32) + offset[start : start + (WIDTH << target), :]
        for source in range(4):
            if source < target:
                share = 0.25 ** (target - source)
                shrunk = jnp.dot(maps[source], masks[source, target], preferred_element_type=F32)
                term = mixed(weight_ref, target, source, (shrunk * share).astype(BF16))
                total = total + term.astype(F32)
            elif source > target:
                term = mixed(weight_ref, target, source, maps[source])
                total = total + lax.dot_general(
                    term,
                    masks[target, source],
                    (((1,), (1,)), ((), ())),
                    preferred_element_type=F32,
                )
        total = jnp.maximum(total, 0.0)
        out_ref = out_refs[target]
        if len(out_ref.shape) == 2:
            out_ref[...] = total.T.astype(BF16)
        else:
            lines = [total[:, at : at + LANES] for at in range(0, total.shape[1], LANES)]
            out_ref[...] = jnp.stack(lines, axis=1).astype(BF16)


def join_kernel(held0, held1, held2, held3, weight_ref, bias_ref, *out_refs):
    masks = {
        (fine, coarse): block_mask(fine, coarse)
        for fine in range(3)
        for coarse in range(fine + 1, 4)
    }
    total = bias_ref.shape[1]
    line = jnp.concatenate([bias_ref[...], jnp.zeros((1, -total % LANES), F32)], axis=1)
    offset = jnp.broadcast_to(line, (8, line.shape[1])).T[:total, 0:1]
    third = held2[...].astype(F32)
    odd = lax.rem(lax.axis_index("row"), 2) == 1
    third = jnp.where(odd, turned(third, 64), third).astype(BF16)[:, :64]
    last = held3[...].astype(F32)
    last = jnp.concatenate([turned(last, -16 * g) for g in range(8)], axis=0)
    maps = [held0[...], held1[...], third, last.astype(BF16)[:, :16]]
    join_strip(maps, masks, weight_ref, offset, out_refs)


def joined(helds, join_weight, join_bias):
    vmem = pl.BlockSpec(memory_space=pltpu.VMEM)
    shapes = [(WIDTH << b, (TH >> b) // STRIPS, TW >> b) for b in range(4)]
    outs = pl.pallas_call(
        join_kernel,
        out_shape=[
            jax.ShapeDtypeStruct(
                shape if shape[2] == LANES else (shape[1] * shape[2], shape[0]), BF16
            )
            for shape in shapes
        ],
        in_specs=[vmem] * 6,
        out_specs=[vmem] * 4,
        name="join",
    )(*helds, join_weight, join_bias[None, :])
    return tuple(
        out if out.ndim == 3 else out.reshape(*shape[1:], shape[0]).transpose(2, 0, 1)
        for out, shape in zip(outs, shapes)
    )


def local(section_in, conv_weight, conv_bias, join_weight, join_bias):
    helds = front(section_in[0, 0, 0], conv_weight[0], conv_bias[0])
    return joined(helds, join_weight, join_bias)


def solution(mesh):
    in_specs = (
        P("branch", "row", "col", None, None),
        P("branch", None, None, None, None, None),
        P("branch", None, None),
        P(),
        P(),
    )
    out_specs = (P(None, ("branch", "row"), "col"),) * 4
    return jax.shard_map(local, mesh=mesh, in_specs=in_specs, out_specs=out_specs, check_vma=False)
```

time: 42.2 us -> 35.3 us (0.84)
  the two profiles are of different devices: /device:TPU:0 before, /device:TPU:29 now
where the time goes in v1:
time: 35.3 us; the launch traced here: 35.1 us
  Pallas kernels  33.1 us (94%)
  local copies, waits for them, and re-layouts  1.28 us (4%)
  between operations  0.64 us (2%)
    pallas_call x1, Pallas kernels, front(): pl.pallas_call(front_kernel, out_shape=[jax.ShapeDtypeStruct(shape, BF16)...  28.8 us
    pallas_call x1, Pallas kernels, joined(): pl.pallas_call(join_kernel, out_shape=[jax.ShapeDtypeStruct(shape if shap...  4.3 us
    broadcast_in_dim x1, local copies, waits for them, and re-layouts, joined(): join_bias[None, :]  1.28 us

profile of v1, /device:TPU:29, one launch (start us, length us, event | category | flops | bytes accessed | tf_op | source)
XLA Modules:
  0.0 35.1 jit_solution(10218345644402659650)
XLA Ops:
  0.6 1.3 %broadcast_in_dim.3.bias_ref = f32[1,720]{1,0:T(1,128)} reshape(f32[720]{0:T(1024)} %param.9) | data formatting | bytes 5760 | tf_op jit(solution)/shard_map/broadcast_in_dim | solution.py:540
  1.9 28.8 %front.1 = (bf16[48,1024]{1,0:T(8,128)(2,1)}, bf16[96,256]{1,0:T(8,128)(2,1)}, bf16[192,128]{1,0:T(8,128)(2,1)}, bf16[48,128]{1,0:T(8,128)(2,1)}) custom-call(bf16[48,4096]{1,0:T(8,128)(2,1)} %bitcast.13, bf16[2,3,3,384,384]{4,3,2,1,0:T(8,128)(2,1)} %bitcast.12, f32[2,384]{1,0:T(2,128)} %bitcast.14), custom_call_target="tpu_custom_call" | custom-call | tf_op jit(solution)/shard_map/front/pallas_call | solution.py:434
  30.8 4.3 %join.1 = (bf16[48,8,128]{2,1,0:T(8,128)(2,1)}, bf16[256,96]{1,0:T(8,128)(2,1)}, bf16[64,192]{1,0:T(8,128)(2,1)}, bf16[16,384]{1,0:T(8,128)(2,1)}) custom-call(bf16[48,1024]{1,0:T(8,128)(2,1)} %get-tuple-element.12.held0, bf16[96,256]{1,0:T(8,128)(2,1)} %get-tuple-element.13.held1, bf16[192,128]{1,0:T(8,128)(2,1)} %get-tuple-element.14.held2, ...), custom_call_target="tpu_custom_call" | custom-call | tf_op jit(solution)/shard_map/join/pallas_call | solution.py:529

commit v2 on v1

--- a/solution.py
+++ b/solution.py
@@ -21,6 +21,36 @@
 BEFORE = (2, 1, 1, 0)
 FIELD_TILES = (36, 10, 4, 1)
 HIDDEN_TILES = (34, 10, 4, 1)
+
+
+CHUNKS = (4, 2, 2, 1)
+RELAYS = 12
+
+
+def route(source, tile, strip, chunk):
+    if tile == source or strip == tile:
+        return None
+    if source == 0 and strip == 3 - tile and chunk % 2 == 0:
+        return None
+    return strip
+
+
+def relayed(source, place):
+    pieces = [
+        (tile, strip, chunk)
+        for chunk in range(CHUNKS[source])
+        for tile in range(STRIPS)
+        for strip in range(STRIPS)
+        if tile != place and route(source, tile, strip, chunk) == place
+    ]
+    return sorted(pieces, key=lambda p: (p[2], (p[0] ^ place).bit_count(), -abs(p[0] - source)))
+
+
+def own_pieces(source, place):
+    chunks = range(CHUNKS[source])
+    if source == place:
+        return [(place ^ turn, chunk) for turn in (0, 1, 2, 3) for chunk in chunks]
+    return [(place ^ turn, chunk) for chunk in chunks for turn in (1, 2, 0, 3)]
 
 
 def lane_index(width=LANES):
@@ -137,8 +167,8 @@
     section, kernels, biases, held0, held1, held2, held3,
     container, weights, bias, own0, own1, own2, own3, side0, side1, side2, side3,
     pack_send, pack_recv, hide0, hide1, hide2, hide3, hid0, hid1, hid2, hid3,
-    settled0, settled1, settled2, settled3, load_sem,
-    halo_send, halo_recv, hidden_send, hidden_recv, strip_send, strip_recv, own_sem,
+    settled0, settled1, settled2, settled3, relay0, relay1, relay2, relay3, load_sem,
+    halo_send, halo_recv, hidden_send, hidden_recv, strip_send, strip_recv, relay_recv, own_sem,
 ):
     level = lax.axis_index("branch")
     place = lax.axis_index("row")
@@ -171,15 +201,18 @@
             pl.semaphore_signal(barrier, inc=1, device_id=device, device_id_type=MESH)
 
     at_home = level == place
-    for source in range(STRIPS):
-
-        @pl.when(jnp.logical_not(at_home & (level == source)))
-        def _():
-            pl.semaphore_signal(
-                barrier, inc=1, device_id=(source, level, col), device_id_type=MESH
-            )
-
-    expected = expected + STRIPS - at_home.astype(jnp.int32)
+    for step in range(1, STRIPS):
+        for device in (
+            (level, lax.rem(place + step, STRIPS), col),
+            (lax.rem(level + step, STRIPS), place, col),
+        ):
+            pl.semaphore_signal(barrier, inc=1, device_id=device, device_id_type=MESH)
+
+    @pl.when((level > 0) & (place == STRIPS - 1 - level))
+    def _():
+        pl.semaphore_signal(barrier, inc=1, device_id=(0, level, col), device_id_type=MESH)
+
+    expected = expected + 2 * (STRIPS - 1) + ((level == 0) & (place > 0)).astype(jnp.int32)
 
     helds = (held0, held1, held2, held3)
     owns = (own0, own1, own2, own3)
@@ -187,13 +220,14 @@
     hides = (hide0, hide1, hide2, hide3)
     hids = (hid0, hid1, hid2, hid3)
     settleds = (settled0, settled1, settled2, settled3)
+    relays = (relay0, relay1, relay2, relay3)
 
     def run(b):
         channels = WIDTH << b
         width = -(-channels // LANES) * LANES
         cols, rows = TW >> b, TH >> b
         own, side, hide, hid = owns[b], sides[b], hides[b], hids[b]
-        settled, held = settleds[b], helds[b]
+        settled, held, relay = settleds[b], helds[b], relays[b]
         before, tiles = BEFORE[b], OWN_TILES[b]
         middle = slice(before * LANES, (before + tiles) * LANES)
 
@@ -219,15 +253,19 @@
         load.wait()
         if b:
             own[:, middle] = natural_tile(b, container)
-        packed = b == 3
+        packed = b >= 2
         lane = lane_index()
+        folds = (WIDTH << b) // 96
+        pair = 2 * cols
         if packed:
-            whole = own[...].astype(F32)
             for end in range(2):
+                tile = before if end == 0 else before + tiles - 1
+                at = 0 if end == 0 else (rows - 2) * cols % LANES
+                edge = own[:, tile * LANES : (tile + 1) * LANES].astype(F32)
                 out = None
-                for g in range(4):
-                    part = turned(whole[g * 96 : (g + 1) * 96], 32 * g - 32 * end)
-                    out = part if g == 0 else jnp.where(lane < 32 * g, out, part)
+                for g in range(folds):
+                    part = turned(edge[g * 96 : (g + 1) * 96], pair * g - at)
+                    out = part if g == 0 else jnp.where(lane < pair * g, out, part)
                 pack_send[end] = out.astype(BF16)
 
         def halo_region(dr, dc):
@@ -279,19 +317,27 @@
         for dr, dc in order:
             pl.when(reach(-dr, -dc)[0])(halo_copy(dr, dc).wait_recv)
 
-        fields = [own[...], side[0], side[1]]
+        fields = [own, side.at[0], side.at[1]]
         if packed:
             for at, dc in enumerate((0, 1, -1)):
                 upper = pack_recv[WAYS.index((1, dc))].astype(F32)
                 lower = pack_recv[WAYS.index((-1, dc))].astype(F32)
                 lines = []
-                for g in range(4):
-                    here = fields[at][g * 96 : (g + 1) * 96].astype(F32)
-                    ring = jnp.where(
-                        lane < 96, turned(lower, 64 - 32 * g), turned(upper, 96 - 32 * g)
-                    )
-                    lines.append(jnp.where(lane < 64, here, ring).astype(BF16))
+                for g in range(folds):
+                    span = slice(g * 96, (g + 1) * 96)
+                    here = fields[at][span, middle]
+                    above = turned(upper, LANES - pair - pair * g)
+                    if b == 3:
+                        ring = jnp.where(lane < 96, turned(lower, 64 - pair * g), above)
+                        lines.append(jnp.where(lane < 64, here.astype(F32), ring).astype(BF16))
+                    else:
+                        below = turned(lower, -pair * g)
+                        lines.append(
+                            jnp.concatenate([above.astype(BF16), here, below.astype(BF16)], axis=1)
+                        )
                 fields[at] = jnp.concatenate(lines, axis=0)
+        else:
+            fields = [field[...] for field in fields]
 
         products = jnp.dot(
             taps(b, weights, 0),
@@ -351,46 +397,73 @@
                     out = part if g == 0 else jnp.where(lane < 16 * g, out, part)
                 settled[strip] = out.astype(BF16)
 
-        def strip_source(strip):
+        chunks = CHUNKS[b]
+
+        def ends(strip, chunk):
             if b == 3:
-                return settled.at[strip]
+                return settled.at[strip], held
             if b == 2:
-                return settled.at[:, pl.ds(pl.multiple_of(strip // 2 * LANES, LANES), LANES)]
-            size = tiles * LANES // STRIPS
-            return settled.at[:, pl.ds(pl.multiple_of(strip * size, LANES), size)]
-
-        def strip_copies(turn):
-            strip = lax.rem(place + turn, STRIPS)
-            source = strip_source(strip)
-            remote = pltpu.make_async_remote_copy(
+                size = channels // chunks
+                span = slice(chunk * size, (chunk + 1) * size)
+                tile = strip // 2
+                return settled.at[span, tile * LANES : (tile + 1) * LANES], held.at[span]
+            size = tiles * LANES // STRIPS // chunks
+            at = (strip * chunks + chunk) * size
+            return settled.at[:, at : at + size], held.at[:, chunk * size : (chunk + 1) * size]
+
+        def send(source, target, semaphore, arrived, device):
+            copy = pltpu.make_async_remote_copy(
                 src_ref=source,
-                dst_ref=held,
-                send_sem=strip_send.at[turn],
-                recv_sem=strip_recv.at[b],
-                device_id=(place, strip, col),
+                dst_ref=target,
+                send_sem=strip_send.at[semaphore],
+                recv_sem=arrived,
+                device_id=device,
                 device_id_type=MESH,
             )
-            return remote, pltpu.make_async_copy(source, held, own_sem)
-
-        for turn in range(STRIPS):
-            remote, local_copy = strip_copies(turn)
-            if turn == 0:
-                pl.when(jnp.logical_not(at_home))(remote.start)
-                pl.when(at_home)(local_copy.start)
-            else:
-                remote.start()
+            copy.start()
+            return copy.wait_send
+
+        def exchange(here):
+            waits = []
+            for strip, chunk in own_pieces(b, here):
+                source, target = ends(strip, chunk)
+                if here == b and strip == here:
+                    copy = pltpu.make_async_copy(source, target, own_sem.at[chunk])
+                    copy.start()
+                    waits.append(copy.wait)
+                    continue
+                via = route(b, here, strip, chunk)
+                if via is None:
+                    arrived, device = strip_recv.at[b], (here, strip, col)
+                else:
+                    slot = relayed(b, via).index((here, strip, chunk))
+                    target = relay.at[slot]
+                    arrived, device = relay_recv.at[slot], (b, via, col)
+                waits.append(send(source, target, len(waits), arrived, device))
+            for slot, (tile, strip, chunk) in enumerate(relayed(b, here)):
+                piece = relay.at[slot]
+                pltpu.make_async_remote_copy(
+                    src_ref=piece,
+                    dst_ref=piece,
+                    send_sem=strip_send.at[0],
+                    recv_sem=relay_recv.at[slot],
+                    device_id=(b, tile, col),
+                    device_id_type=MESH,
+                ).wait_recv()
+                target = ends(strip, chunk)[1]
+                waits.append(
+                    send(piece, target, len(waits), strip_recv.at[b], (tile, strip, col))
+                )
+            for wait in waits:
+                wait()
+
+        for here in range(STRIPS):
+            pl.when(place == here)(partial(exchange, here))
 
         for dr, dc in order:
             pl.when(reach(dr, dc)[0])(halo_copy(dr, dc).wait_send)
         for dc in (1, -1):
             pl.when(reach(0, dc)[0])(hidden_copy(dc).wait_send)
-        for turn in range(STRIPS):
-            remote, local_copy = strip_copies(turn)
-            if turn == 0:
-                pl.when(jnp.logical_not(at_home))(remote.wait_send)
-                pl.when(at_home)(local_copy.wait)
-            else:
-                remote.wait_send()
 
     for b in range(STRIPS):
         pl.when(level == b)(partial(run, b))
@@ -429,8 +502,10 @@
     scratch += [pltpu.VMEM(field(b, HIDDEN_TILES), BF16) for b in range(4)]
     scratch += [pltpu.VMEM(field(b, OWN_TILES), BF16) for b in range(3)]
     scratch += [pltpu.VMEM((STRIPS, WIDTH, LANES), BF16)]
-    dma = pltpu.SemaphoreType.DMA
-    scratch += [dma((4,)), dma((8,)), dma((8,)), dma((2,)), dma((2,)), dma((4,)), dma((4,)), dma]
+    pieces = ((48, 256), (96, 128), (96, 128), (48, 128))
+    scratch += [pltpu.VMEM((RELAYS, *piece), BF16) for piece in pieces]
+    counts = (4, 8, 8, 2, 2, 16 + RELAYS, 4, RELAYS, 4)
+    scratch += [pltpu.SemaphoreType.DMA((count,)) for count in counts]
     return pl.pallas_call(
         front_kernel,
         out_shape=[jax.ShapeDtypeStruct(shape, BF16) for shape in HELD_SHAPES],
@@ -511,8 +586,8 @@
         for fine in range(3)
         for coarse in range(fine + 1, 4)
     }
-    total = bias_ref.shape[1]
-    line = jnp.concatenate([bias_ref[...], jnp.zeros((1, -total % LANES), F32)], axis=1)
+    total = bias_ref.shape[0]
+    line = jnp.concatenate([bias_ref[...][None, :], jnp.zeros((1, -total % LANES), F32)], axis=1)
     offset = jnp.broadcast_to(line, (8, line.shape[1])).T[:total, 0:1]
     third = held2[...].astype(F32)
     odd = lax.rem(lax.axis_index("row"), 2) == 1
@@ -537,7 +612,7 @@
         in_specs=[vmem] * 6,
         out_specs=[vmem] * 4,
         name="join",
-    )(*helds, join_weight, join_bias[None, :])
+    )(*helds, join_weight, join_bias)
     return tuple(
         out if out.ndim == 3 else out.reshape(*shape[1:], shape[0]).transpose(2, 0, 1)
         for out, shape in zip(outs, shapes)

time: 35.3 us -> 26.8 us (0.76)
  the two profiles are of different devices: /device:TPU:29 before, /device:TPU:0 now
where the time goes in v2:
time: 26.8 us; the launch traced here: 26.6 us
  Pallas kernels  26 us (97%)
  between operations  0.64 us (2%)
    pallas_call x1, Pallas kernels, front(): pl.pallas_call(front_kernel, out_shape=[jax.ShapeDtypeStruct(shape, BF16)...  21.7 us
    pallas_call x1, Pallas kernels, joined(): pl.pallas_call(join_kernel, out_shape=[jax.ShapeDtypeStruct(shape if shap...  4.31 us

profile of v2, /device:TPU:0, one launch (start us, length us, event | category | flops | bytes accessed | tf_op | source)
XLA Modules:
  0.0 26.6 jit_solution(4563490091812134885)
XLA Ops:
  0.6 21.7 %front.1 = (bf16[48,1024]{1,0:T(8,128)(2,1)}, bf16[96,256]{1,0:T(8,128)(2,1)}, bf16[192,128]{1,0:T(8,128)(2,1)}, bf16[48,128]{1,0:T(8,128)(2,1)}) custom-call(bf16[48,4096]{1,0:T(8,128)(2,1)} %bitcast.13, bf16[2,3,3,384,384]{4,3,2,1,0:T(8,128)(2,1)} %bitcast.12, f32[2,384]{1,0:T(2,128)} %bitcast.14), custom_call_target="tpu_custom_call" | custom-call | tf_op jit(solution)/shard_map/front/pallas_call | solution.py:509
  22.3 4.3 %join.1 = (bf16[48,8,128]{2,1,0:T(8,128)(2,1)}, bf16[256,96]{1,0:T(8,128)(2,1)}, bf16[64,192]{1,0:T(8,128)(2,1)}, bf16[16,384]{1,0:T(8,128)(2,1)}) custom-call(bf16[48,1024]{1,0:T(8,128)(2,1)} %get-tuple-element.12.held0, bf16[96,256]{1,0:T(8,128)(2,1)} %get-tuple-element.13.held1, bf16[192,128]{1,0:T(8,128)(2,1)} %get-tuple-element.14.held2, ...), custom_call_target="tpu_custom_call" | custom-call | tf_op jit(solution)/shard_map/join/pallas_call | solution.py:604

commit v3 on v2

v3 whole, which is shorter than its diff:
```python
from functools import partial

import jax
import jax.numpy as jnp
from jax import lax
from jax.experimental import pallas as pl
from jax.experimental.pallas import tpu as pltpu
from jax.sharding import PartitionSpec as P

WIDTH = 48
TH = 32
TW = 128
LANES = 128
STRIPS = 4
MESH = pl.DeviceIdType.MESH
WAYS = [(dr, dc) for dr in (-1, 0, 1) for dc in (-1, 0, 1) if dr or dc]
F32 = jnp.float32
BF16 = jnp.bfloat16

OWN_TILES = (32, 8, 2, 1)
BEFORE = (2, 1, 1, 0)
FIELD_TILES = (36, 10, 4, 1)
HIDDEN_TILES = (34, 10, 4, 1)


CHUNKS = (4, 2, 2, 1)
RELAYS = 12


def route(source, tile, strip, chunk):
    if tile == source or strip == tile:
        return None
    if source == 0 and strip == 3 - tile and chunk % 2 == 0:
        return None
    return strip


def relayed(source, place):
    pieces = [
        (tile, strip, chunk)
        for chunk in range(CHUNKS[source])
        for tile in range(STRIPS)
        for strip in range(STRIPS)
        if tile != place and route(source, tile, strip, chunk) == place
    ]
    return sorted(pieces, key=lambda p: (p[2], (p[0] ^ place).bit_count(), -abs(p[0] - source)))


def own_pieces(source, place):
    chunks = range(CHUNKS[source])
    if source == place:
        return [(place ^ turn, chunk) for turn in (0, 1, 2, 3) for chunk in chunks]
    return [(place ^ turn, chunk) for chunk in chunks for turn in (1, 2, 0, 3)]


def lane_index(width=LANES):
    return lax.broadcasted_iota(jnp.int32, (1, width), 1)


def turned(group, shift):
    shift = shift % LANES
    return pltpu.roll(group, shift, 1) if shift else group


def tiles_turned(field, shift):
    if shift % LANES == 0:
        return field
    tiles = [turned(field[:, t : t + LANES], shift) for t in range(0, field.shape[1], LANES)]
    return tiles[0] if len(tiles) == 1 else jnp.concatenate(tiles, axis=1)


def natural_tile(branch_level, container_ref):
    pixels = TH * TW >> 2 * branch_level
    channels = WIDTH << branch_level
    parts = []
    for part in range(1 << branch_level):
        at = part * pixels
        low = at // LANES * LANES
        piece = container_ref[:, low : low + max(pixels, LANES)]
        if at > low:
            piece = pltpu.roll(piece.astype(F32), LANES - at + low, 1).astype(BF16)
        parts.append(piece)
    held = lax.broadcasted_iota(jnp.int32, (1, channels), 1)
    part = sum((held >= WIDTH * turn).astype(jnp.int32) for turn in range(1, 1 << branch_level))
    home = ((held - WIDTH * part) << branch_level) + part
    order = jnp.where(lax.broadcasted_iota(jnp.int32, (channels, channels), 0) == home, 1.0, 0.0)
    return jnp.dot(
        order.astype(BF16), jnp.concatenate(parts, axis=0), preferred_element_type=F32
    ).astype(BF16)


def column_stack(branch_level, own, west, east):
    cols = TW >> branch_level
    col = lane_index(own.shape[1]) & (cols - 1)
    own32 = own.astype(F32)
    minus = tiles_turned(
        jnp.where(col == cols - 1, tiles_turned(west.astype(F32), -cols), own32), 1
    ).astype(BF16)
    plus = tiles_turned(
        jnp.where(col == 0, tiles_turned(east.astype(F32), cols), own32), -1
    ).astype(BF16)

    def zeros(rows):
        return jnp.zeros((rows, own.shape[1]), BF16)

    if branch_level == 0:
        pieces = [minus, own, zeros(32), plus, zeros(80)]
    elif branch_level == 3:
        pieces = [minus, own, plus]
    else:
        pad = zeros(-own.shape[0] % LANES)
        pieces = [minus, pad, own, pad, plus, pad]
    return jnp.concatenate(pieces, axis=0)


def taps(branch_level, weights, layer):
    channels = WIDTH << branch_level
    width = -(-channels // LANES) * LANES
    lines = []
    for dy in range(3):
        if branch_level == 0:
            first, middle, last = (weights[layer, dy, dx, 0:channels, 0:width] for dx in range(3))
            pair = jnp.where(
                lane_index() < channels,
                first.astype(F32),
                pltpu.roll(middle.astype(F32), channels, 1),
            )
            lines.append(jnp.concatenate([pair.astype(BF16), last], axis=1))
        else:
            lines.append(
                jnp.concatenate(
                    [weights[layer, dy, dx, 0:channels, 0:width] for dx in range(3)], axis=1
                )
            )
    return jnp.concatenate(lines, axis=0)


def row_sum(branch_level, products, first, count):
    channels = products.shape[0] // 3
    cols = TW >> branch_level
    above, here, below = (products[d * channels : (d + 1) * channels] for d in range(3))
    span = slice(first * LANES, (first + count) * LANES)
    if cols == LANES:
        return (
            above[:, (first - 1) * LANES : (first - 1 + count) * LANES]
            + here[:, span]
            + below[:, (first + 1) * LANES : (first + 1 + count) * LANES]
        )
    last = products.shape[1] // LANES - 1
    above, below = tiles_turned(above, cols), tiles_turned(below, -cols)
    lane = lane_index()

    def tile(field, t):
        t = min(max(t, 0), last)
        return field[:, t * LANES : (t + 1) * LANES]

    tiles = [
        jnp.where(lane < cols, tile(above, t - 1), tile(above, t))
        + tile(here, t)
        + jnp.where(lane >= LANES - cols, tile(below, t + 1), tile(below, t))
        for t in range(first, first + count)
    ]
    return tiles[0] if count == 1 else jnp.concatenate(tiles, axis=1)


def front_kernel(
    section, kernels, biases, join_weight, join_bias, out0, out1, out2, out3,
    held0, held1, held2, held3, mix, mix_bias, pool0, pool1, pool2,
    container, weights, bias, own0, own1, own2, own3, side0, side1, side2, side3,
    pack_send, pack_recv, hide0, hide1, hide2, hide3, hid0, hid1, hid2, hid3,
    settled0, settled1, settled2, settled3, relay0, relay1, relay2, relay3, load_sem,
    halo_send, halo_recv, hidden_send, hidden_recv, strip_send, strip_recv, relay_recv, own_sem,
):
    level = lax.axis_index("branch")
    place = lax.axis_index("row")
    col = lax.axis_index("col")
    row_count = lax.axis_size("row")
    col_count = lax.axis_size("col")

    def reach(dr, dc):
        there = jnp.bool_(True)
        if dr:
            there = (place + dr >= 0) & (place + dr < row_count)
        if dc:
            sideways = (col + dc >= 0) & (col + dc < col_count)
            there = there & sideways if dr else sideways
        device = (
            level,
            lax.rem(place + dr + row_count, row_count),
            lax.rem(col + dc + col_count, col_count),
        )
        return there, device

    barrier = pltpu.get_barrier_semaphore()
    expected = 0
    for dr, dc in WAYS:
        there, device = reach(dr, dc)
        expected = expected + there.astype(jnp.int32)

        @pl.when(there)
        def _():
            pl.semaphore_signal(barrier, inc=1, device_id=device, device_id_type=MESH)

    at_home = level == place
    for step in range(1, STRIPS):
        for device in (
            (level, lax.rem(place + step, STRIPS), col),
            (lax.rem(level + step, STRIPS), place, col),
        ):
            pl.semaphore_signal(barrier, inc=1, device_id=device, device_id_type=MESH)

    @pl.when((level > 0) & (place == STRIPS - 1 - level))
    def _():
        pl.semaphore_signal(barrier, inc=1, device_id=(0, level, col), device_id_type=MESH)

    expected = expected + 2 * (STRIPS - 1) + ((level == 0) & (place > 0)).astype(jnp.int32)

    helds = (held0, held1, held2, held3)
    owns = (own0, own1, own2, own3)
    sides = (side0, side1, side2, side3)
    hides = (hide0, hide1, hide2, hide3)
    hids = (hid0, hid1, hid2, hid3)
    settleds = (settled0, settled1, settled2, settled3)
    relays = (relay0, relay1, relay2, relay3)

    mix_loads = [
        pltpu.make_async_copy(join_weight, mix, load_sem.at[4]),
        pltpu.make_async_copy(join_bias, mix_bias, load_sem.at[5]),
    ]

    def branch(b):
        channels = WIDTH << b
        width = -(-channels // LANES) * LANES
        pixels = TH * TW >> b
        cols, rows = TW >> b, TH >> b
        own, side, hide, hid = owns[b], sides[b], hides[b], hids[b]
        settled, held, relay = settleds[b], helds[b], relays[b]
        before, tiles = BEFORE[b], OWN_TILES[b]
        middle = slice(before * LANES, (before + tiles) * LANES)
        packed = b >= 2
        folds = channels // 96
        pair = 2 * cols
        chunks = CHUNKS[b]
        lane = lane_index()
        order = [way for way in WAYS if way[0]] + [way for way in WAYS if not way[0]]

        load = pltpu.make_async_copy(
            section.at[:, 0:pixels],
            own.at[:, middle] if b == 0 else container.at[:, 0:pixels],
            load_sem.at[0],
        )
        bias_load = pltpu.make_async_copy(biases, bias, load_sem.at[1])
        weight_loads = [
            pltpu.make_async_copy(
                kernels.at[layer, :, :, 0:channels, 0:width],
                weights.at[layer, :, :, 0:channels, 0:width],
                load_sem.at[2 + layer],
            )
            for layer in range(2)
        ]

        def begin():
            for copy in (load, bias_load, *weight_loads, *mix_loads):
                copy.start()

        def halo_region(dr, dc):
            if packed and dr:
                return pack_recv.at[WAYS.index((dr, dc))]
            target = own if dc == 0 else side.at[0 if dc == 1 else 1]
            if dr == 0:
                return target.at[:, middle]
            if dr == 1:
                return target.at[:, 0 : before * LANES]
            return target.at[:, (before + tiles) * LANES : (before + tiles + before) * LANES]

        def halo_source(dr):
            if dr == 0:
                return own.at[:, middle]
            if packed:
                return pack_send.at[0 if dr == -1 else 1]
            first = before if dr == -1 else tiles
            return own.at[:, first * LANES : (first + before) * LANES]

        def halo_copy(dr, dc):
            way = WAYS.index((dr, dc))
            return pltpu.make_async_remote_copy(
                src_ref=halo_source(dr),
                dst_ref=halo_region(dr, dc),
                send_sem=halo_send.at[way],
                recv_sem=halo_recv.at[way],
                device_id=reach(dr, dc)[1],
                device_id_type=MESH,
            )

        def hidden_copy(dc):
            at = 0 if dc == 1 else 1
            return pltpu.make_async_remote_copy(
                src_ref=hid,
                dst_ref=hide.at[at],
                send_sem=hidden_send.at[at],
                recv_sem=hidden_recv.at[at],
                device_id=reach(0, dc)[1],
                device_id_type=MESH,
            )

        def ends(strip, chunk):
            if b == 3:
                return settled.at[strip], held
            if b == 2:
                size = channels // chunks
                span = slice(chunk * size, (chunk + 1) * size)
                tile = strip // 2
                return settled.at[span, tile * LANES : (tile + 1) * LANES], held.at[span]
            size = tiles * LANES // STRIPS // chunks
            at = (strip * chunks + chunk) * size
            return settled.at[:, at : at + size], held.at[:, chunk * size : (chunk + 1) * size]

        def exchange(here, closing=False):
            count = 0

            def send(source, target, arrived, device):
                nonlocal count
                copy = pltpu.make_async_remote_copy(
                    src_ref=source,
                    dst_ref=target,
                    send_sem=strip_send.at[count],
                    recv_sem=arrived,
                    device_id=device,
                    device_id_type=MESH,
                )
                count += 1
                if closing:
                    copy.wait_send()
                else:
                    copy.start()

            at_once = []
            for strip, chunk in own_pieces(b, here):
                source, target = ends(strip, chunk)
                if here == b and strip == here:
                    if not closing:
                        copy = pltpu.make_async_copy(source, target, own_sem.at[chunk])
                        copy.start()
                        at_once.append(copy)
                    continue
                via = route(b, here, strip, chunk)
                if via is None:
                    send(source, target, strip_recv.at[b], (here, strip, col))
                else:
                    slot = relayed(b, via).index((here, strip, chunk))
                    send(source, relay.at[slot], relay_recv.at[slot], (b, via, col))
            for slot, (tile, strip, chunk) in enumerate(relayed(b, here)):
                piece = relay.at[slot]
                if not closing:
                    pltpu.make_async_remote_copy(
                        src_ref=piece,
                        dst_ref=piece,
                        send_sem=strip_send.at[0],
                        recv_sem=relay_recv.at[slot],
                        device_id=(b, tile, col),
                        device_id_type=MESH,
                    ).wait_recv()
                send(piece, ends(strip, chunk)[1], strip_recv.at[b], (tile, strip, col))
            for copy in at_once:
                copy.wait()

        def run():
            load.wait()
            if b:
                own[:, middle] = natural_tile(b, container)
            if packed:
                for end in range(2):
                    tile = before if end == 0 else before + tiles - 1
                    at = 0 if end == 0 else (rows - 2) * cols % LANES
                    edge = own[:, tile * LANES : (tile + 1) * LANES].astype(F32)
                    out = None
                    for g in range(folds):
                        part = turned(edge[g * 96 : (g + 1) * 96], pair * g - at)
                        out = part if g == 0 else jnp.where(lane < pair * g, out, part)
                    pack_send[end] = out.astype(BF16)

            pl.semaphore_wait(barrier, expected)
            for dr, dc in order:
                pl.when(reach(dr, dc)[0])(halo_copy(dr, dc).start)
            for dr, dc in order:

                @pl.when(jnp.logical_not(reach(-dr, -dc)[0]))
                def _():
                    region = halo_region(dr, dc)
                    region[...] = jnp.zeros(region.shape, BF16)

            bias_load.wait()
            offsets = [
                jnp.broadcast_to(bias[layer : layer + 1, :], (8, bias.shape[1])).T[:channels, 0:1]
                for layer in range(2)
            ]
            weight_loads[0].wait()
            for dr, dc in order:
                pl.when(reach(-dr, -dc)[0])(halo_copy(dr, dc).wait_recv)

            fields = [own, side.at[0], side.at[1]]
            if packed:
                for at, dc in enumerate((0, 1, -1)):
                    upper = pack_recv[WAYS.index((1, dc))].astype(F32)
                    lower = pack_recv[WAYS.index((-1, dc))].astype(F32)
                    lines = []
                    for g in range(folds):
                        span = slice(g * 96, (g + 1) * 96)
                        here = fields[at][span, middle]
                        above = turned(upper, LANES - pair - pair * g)
                        if b == 3:
                            ring = jnp.where(lane < 96, turned(lower, 64 - pair * g), above)
                            lines.append(jnp.where(lane < 64, here.astype(F32), ring).astype(BF16))
                        else:
                            below = turned(lower, -pair * g)
                            lines.append(
                                jnp.concatenate([above.astype(BF16), here, below.astype(BF16)], axis=1)
                            )
                    fields[at] = jnp.concatenate(lines, axis=0)
            else:
                fields = [field[...] for field in fields]

            products = jnp.dot(
                taps(b, weights, 0),
                column_stack(b, *fields),
                preferred_element_type=F32,
            )
            first = 1 if b == 0 else 0
            hidden = row_sum(b, products, first, HIDDEN_TILES[b])
            hidden = jnp.maximum(hidden + offsets[0], 0.0)
            row = lax.shift_right_logical(lane_index(HIDDEN_TILES[b] * LANES), cols.bit_length() - 1)
            if b == 3:
                row = jnp.where(row >= 6, row - 8, row)
            else:
                row = row - (before - first) * (LANES // cols)
            low = jnp.where(place == 0, 0, -LANES)
            high = jnp.where(place == row_count - 1, rows, 2 * LANES)
            hidden = jnp.where((row >= low) & (row < high), hidden, 0.0)
            hid[...] = hidden.astype(BF16)

            for dc in (1, -1):
                pl.when(reach(0, dc)[0])(hidden_copy(dc).start)
            for dc in (1, -1):

                @pl.when(jnp.logical_not(reach(0, -dc)[0]))
                def _():
                    at = 0 if dc == 1 else 1
                    hide[at] = jnp.zeros(hid.shape, BF16)

            weight_loads[1].wait()
            for dc in (1, -1):
                pl.when(reach(0, -dc)[0])(hidden_copy(dc).wait_recv)
            products = jnp.dot(
                taps(b, weights, 1),
                column_stack(b, hid[...], hide[0], hide[1]),
                preferred_element_type=F32,
            )
            after = row_sum(b, products, 1 if b == 0 else before, tiles)
            final = jnp.maximum(after + offsets[1] + own[:, middle].astype(F32), 0.0)
            if b < 3:
                settled[...] = final.astype(BF16)
            else:
                for strip in range(STRIPS):
                    out = None
                    for g in range(8):
                        part = turned(final[g * WIDTH : (g + 1) * WIDTH], 16 * g - 16 * strip)
                        out = part if g == 0 else jnp.where(lane < 16 * g, out, part)
                    settled[strip] = out.astype(BF16)

            for here in range(STRIPS):
                pl.when(place == here)(partial(exchange, here))

        def close():
            for here in range(STRIPS):
                pl.when(place == here)(partial(exchange, here, True))
            for dr, dc in order:
                pl.when(reach(dr, dc)[0])(halo_copy(dr, dc).wait_send)
            for dc in (1, -1):
                pl.when(reach(0, dc)[0])(hidden_copy(dc).wait_send)

        return begin, run, close

    branches = [branch(b) for b in range(STRIPS)]
    for b, (begin, _, _) in enumerate(branches):
        pl.when(level == b)(begin)

    pool_refs = (pool0, pool1, pool2)
    for fine, pool in enumerate(pool_refs):
        pool[...] = pool_table(fine)

    for b, (_, run, _) in enumerate(branches):
        pl.when(level == b)(run)

    for copy in mix_loads:
        copy.wait()

    def arrived(source):
        arrival = pltpu.make_async_remote_copy(
            src_ref=helds[source],
            dst_ref=helds[source],
            send_sem=strip_send.at[0],
            recv_sem=strip_recv.at[source],
            device_id=(source, level, col),
            device_id_type=MESH,
        )
        pl.when(jnp.logical_not(at_home & (level == source)))(arrival.wait_recv)

    join(place, arrived, helds, mix, mix_bias, pool_refs, (out0, out1, out2, out3))

    for b, (_, _, close) in enumerate(branches):
        pl.when(level == b)(close)


def coarse_home(fine_level, coarse_level):
    fine_cols, coarse_cols = TW >> fine_level, TW >> coarse_level
    shift = coarse_level - fine_level
    pixel = lax.broadcasted_iota(jnp.int32, (strip_pixels(fine_level), 1), 0)
    row = lax.shift_right_logical(pixel, fine_cols.bit_length() - 1 + shift)
    return row * coarse_cols + lax.shift_right_logical(pixel & (fine_cols - 1), shift)


def strip_pixels(branch_level):
    return TH * TW // STRIPS >> 2 * branch_level


def pool_table(fine_level):
    at = 0
    hits = []
    for coarse_level in range(fine_level + 1, STRIPS):
        hits.append((at, at + coarse_home(fine_level, coarse_level)))
        at += strip_pixels(coarse_level)
    tiles = []
    for tile in range(-(-at // LANES)):
        target = lane_index() + tile * LANES
        hit = None
        for first, home in hits:
            same = home == target
            hit = same if hit is None else hit | same
        tiles.append(jnp.where(hit, 1.0, 0.0).astype(BF16))
    table = tiles[0] if len(tiles) == 1 else jnp.concatenate(tiles, axis=1)
    short = max(LANES - table.shape[0], 0)
    if short:
        table = jnp.concatenate([table, jnp.zeros((short, table.shape[1]), BF16)], axis=0)
    return table


def product(mix, rows, source, data):
    start = ((1 << source) - 1) * WIDTH
    stop = start + data.shape[0]
    low = start // LANES * LANES
    high = min(-(-stop // LANES) * LANES, mix.shape[1])
    pieces = [data]
    if start > low:
        pieces.insert(0, jnp.zeros((start - low, data.shape[1]), BF16))
    if high > stop:
        pieces.append(jnp.zeros((high - stop, data.shape[1]), BF16))
    stacked = jnp.concatenate(pieces, axis=0)
    return jnp.dot(
        mix[rows, low:high], stacked, preferred_element_type=F32
    ).astype(BF16).astype(F32)


def spread(term, pool):
    return lax.dot_general(
        term.astype(BF16), pool, (((1,), (1,)), ((), ())), preferred_element_type=F32
    )


def join(place, arrived, helds, mix, mix_bias, pools, outs):
    lane = lane_index()
    total = mix_bias.shape[0]
    line = jnp.concatenate([mix_bias[...][None, :], jnp.zeros((1, -total % LANES), F32)], axis=1)
    offset = jnp.broadcast_to(line, (8, line.shape[1])).T
    starts = [((1 << b) - 1) * WIDTH for b in range(STRIPS + 1)]
    offsets = [offset[starts[b] : starts[b + 1], 0:1] for b in range(STRIPS)]
    one, two, three = (slice(starts[b], starts[b + 1]) for b in range(1, STRIPS))

    arrived(3)
    folded = helds[3][...].astype(F32)
    last = jnp.concatenate([turned(folded, -16 * g) for g in range(8)], axis=0)
    from3 = product(mix, slice(0, starts[3]), 3, last.astype(BF16))

    arrived(2)
    pieces = helds[2][...].astype(F32)
    third = jnp.where(lax.rem(place, 2) == 1, turned(pieces, 64), pieces)
    third16 = third.astype(BF16)
    from2 = product(mix, slice(0, starts[2]), 2, third16)
    shrunk = jnp.dot(third16, pools[2][...], preferred_element_type=F32)
    total3 = last + offsets[3] + product(mix, three, 2, (shrunk * 0.25).astype(BF16))
    total2 = third + offsets[2] + spread(from3[two], pools[2][...])

    def side_by_side(near, far):
        return jnp.where(lane < 64, near, jnp.where(lane < 80, turned(far, 64), 0.0))

    arrived(1)
    second = helds[1][...]
    from1 = product(mix, slice(0, starts[1]), 1, second)
    shrunk = jnp.dot(second, pools[1][...], preferred_element_type=F32)
    shrunk = shrunk * jnp.where(lane < 64, 0.25, 0.0625)
    down1 = product(mix, slice(starts[2], total), 1, shrunk.astype(BF16))
    total2 = total2 + down1[: starts[3] - starts[2]]
    tail3 = down1[starts[3] - starts[2] :]
    total1 = second.astype(F32) + offsets[1]
    total1 = total1 + spread(side_by_side(from2[one], from3[one]), pools[1][...])
    first = slice(0, starts[1])
    total0 = offsets[0] + spread(
        jnp.concatenate([from1, side_by_side(from2[first], from3[first])], axis=1), pools[0][...]
    )

    arrived(0)
    maps = helds[0][...]
    shrunk = jnp.dot(maps, pools[0][...], preferred_element_type=F32)
    near = (shrunk[:, :256] * 0.25).astype(BF16)
    far = (shrunk[:, 256:] * jnp.where(lane < 64, 0.0625, 0.015625)).astype(BF16)
    total1 = total1 + product(mix, one, 0, near)
    down0 = product(mix, slice(starts[2], total), 0, far)
    total2 = total2 + down0[: starts[3] - starts[2]]
    total3 = total3 + turned(tail3 + down0[starts[3] - starts[2] :], -64)
    total0 = jnp.maximum(total0 + maps.astype(F32), 0.0)
    lines = [total0[:, at : at + LANES] for at in range(0, total0.shape[1], LANES)]
    outs[0][...] = jnp.stack(lines, axis=1).astype(BF16)
    for out, value in zip(outs[1:], (total1, total2, total3)):
        out[...] = jnp.maximum(value, 0.0).T[: out.shape[0]].astype(BF16)


HELD_SHAPES = ((48, 1024), (96, 256), (192, 128), (48, 128))


def front(section, kernels, biases, join_weight, join_bias):
    anywhere = pl.BlockSpec(memory_space=pl.ANY)
    vmem = pl.BlockSpec(memory_space=pltpu.VMEM)

    def field(b, tiles):
        return (WIDTH << b, tiles[b] * LANES)

    scratch = [pltpu.VMEM(shape, BF16) for shape in HELD_SHAPES]
    scratch += [pltpu.VMEM(join_weight.shape, BF16), pltpu.VMEM(join_bias.shape, F32)]
    scratch += [pltpu.VMEM(shape, BF16) for shape in ((1024, 384), (256, 128), (128, 128))]
    scratch += [
        pltpu.VMEM((WIDTH, TH * TW // 2), BF16),
        pltpu.VMEM(kernels.shape, BF16),
        pltpu.VMEM(biases.shape, F32),
    ]
    scratch += [pltpu.VMEM(field(b, FIELD_TILES), BF16) for b in range(4)]
    scratch += [pltpu.VMEM((2, *field(b, FIELD_TILES)), BF16) for b in range(4)]
    scratch += [pltpu.VMEM((2, 96, LANES), BF16), pltpu.VMEM((8, 96, LANES), BF16)]
    scratch += [pltpu.VMEM((2, *field(b, HIDDEN_TILES)), BF16) for b in range(4)]
    scratch += [pltpu.VMEM(field(b, HIDDEN_TILES), BF16) for b in range(4)]
    scratch += [pltpu.VMEM(field(b, OWN_TILES), BF16) for b in range(3)]
    scratch += [pltpu.VMEM((STRIPS, WIDTH, LANES), BF16)]
    pieces = ((48, 256), (96, 128), (96, 128), (48, 128))
    scratch += [pltpu.VMEM((RELAYS, *piece), BF16) for piece in pieces]
    counts = (6, 8, 8, 2, 2, 16 + RELAYS, 4, RELAYS, 4)
    scratch += [pltpu.SemaphoreType.DMA((count,)) for count in counts]
    return pl.pallas_call(
        front_kernel,
        out_shape=[pltpu.VMEM(shape, BF16) for shape in OUT_SHAPES],
        in_specs=[anywhere] * 5,
        out_specs=[vmem] * 4,
        scratch_shapes=scratch,
        compiler_params=pltpu.CompilerParams(
            collective_id=0, has_side_effects=True, vmem_limit_bytes=VMEM_LIMIT
        ),
        name="front",
    )(
        *(
            pltpu.with_memory_space_constraint(array, pltpu.HBM)
            for array in (section, kernels, biases, join_weight, join_bias)
        )
    )


OUT_SHAPES = ((48, 8, 128), (256, 96), (64, 192), (16, 384))
VMEM_LIMIT = 48 << 20


def finish_kernel(*refs):
    sources, targets, sem = refs[:4], refs[4:8], refs[8]
    copies = [
        pltpu.make_async_copy(source, target, sem.at[at])
        for at, (source, target) in enumerate(zip(sources, targets))
    ]
    for copy in copies:
        copy.start()
    for copy in copies:
        copy.wait()


def finished(outs):
    return pl.pallas_call(
        finish_kernel,
        out_shape=[jax.ShapeDtypeStruct(out.shape, out.dtype) for out in outs],
        in_specs=[pl.BlockSpec(memory_space=pltpu.VMEM)] * 4,
        out_specs=[pl.BlockSpec(memory_space=pl.ANY)] * 4,
        scratch_shapes=[pltpu.SemaphoreType.DMA((4,))],
        compiler_params=pltpu.CompilerParams(vmem_limit_bytes=1 << 20),
        name="finish",
    )(*outs)


def local(section_in, conv_weight, conv_bias, join_weight, join_bias):
    outs = finished(
        front(section_in[0, 0, 0], conv_weight[0], conv_bias[0], join_weight, join_bias)
    )
    shapes = [(WIDTH << b, (TH >> b) // STRIPS, TW >> b) for b in range(4)]
    return tuple(
        out if out.ndim == 3 else out.reshape(*shape[1:], shape[0]).transpose(2, 0, 1)
        for out, shape in zip(outs, shapes)
    )


def solution(mesh):
    in_specs = (
        P("branch", "row", "col", None, None),
        P("branch", None, None, None, None, None),
        P("branch", None, None),
        P(),
        P(),
    )
    out_specs = (P(None, ("branch", "row"), "col"),) * 4
    return jax.shard_map(local, mesh=mesh, in_specs=in_specs, out_specs=out_specs, check_vma=False)
```

time: 26.8 us -> 22.7 us (0.85)
  the two profiles are of different devices: /device:TPU:0 before, /device:TPU:24 now
where the time goes in v3:
time: 22.7 us; the launch traced here: 22.6 us
  Pallas kernels  21.9 us (96%)
  between operations  0.64 us (3%)
    pallas_call x1, Pallas kernels, front(): pl.pallas_call(front_kernel, out_shape=[pltpu.VMEM(shape, BF16) for shape...  21.2 us
    pallas_call x1, Pallas kernels, finished(): pl.pallas_call(finish_kernel, out_shape=[jax.ShapeDtypeStruct(out.shape,...  0.71 us

profile of v3, /device:TPU:24, one launch (start us, length us, event | category | flops | bytes accessed | tf_op | source)
XLA Modules:
  0.0 22.6 jit_solution(11671453444898305998)
XLA Ops:
  0.6 21.2 %front.1 = (bf16[48,8,128]{2,1,0:T(8,128)(2,1)S(1)}, bf16[256,96]{1,0:T(8,128)(2,1)S(1)}, bf16[64,192]{1,0:T(8,128)(2,1)S(1)}, bf16[16,384]{1,0:T(8,128)(2,1)S(1)}) custom-call(bf16[48,4096]{1,0:T(8,128)(2,1)} %bitcast.13, bf16[2,3,3,384,384]{4,3,2,1,0:T(8,128)(2,1)} %bitcast.12, f32[2,384]{1,0:T(2,128)} %bitcast.14, bf16[720,720]{1,0:T(8,128)(2,1)} %join_weight.1, ...), custom_call_target="tpu_custom_call" | custom-call | tf_op jit(solution)/shard_map/front/pallas_call | solution.py:655
  21.9 0.7 %finish.1 = (bf16[48,8,128]{2,1,0:T(8,128)(2,1)}, bf16[256,96]{1,0:T(8,128)(2,1)}, bf16[64,192]{1,0:T(8,128)(2,1)}, bf16[16,384]{1,0:T(8,128)(2,1)}) custom-call(bf16[48,8,128]{2,1,0:T(8,128)(2,1)S(1)} %get-tuple-element.12.refs_0_, bf16[256,96]{1,0:T(8,128)(2,1)S(1)} %get-tuple-element.13.refs_1_, bf16[64,192]{1,0:T(8,128)(2,1)S(1)} %get-tuple-element.14.refs_2_, ...), custom_call_target="tpu_custom_call" | custom-call | tf_op jit(solution)/shard_map/finish/pallas_call | solution.py:690

commit v4 on v3

--- a/solution.py
+++ b/solution.py
@@ -21,6 +21,7 @@
 BEFORE = (2, 1, 1, 0)
 FIELD_TILES = (36, 10, 4, 1)
 HIDDEN_TILES = (34, 10, 4, 1)
+HIDDEN_START = (1, 0, 0, 0)
 
 
 CHUNKS = (4, 2, 2, 1)
@@ -292,16 +293,75 @@
                 device_id_type=MESH,
             )
 
-        def hidden_copy(dc):
+        last = HIDDEN_TILES[b]
+        if b < 2:
+            hidden_parts = ((2, last - 2), (0, 2), (last - 2, last))
+        else:
+            hidden_parts = ((0, last),)
+
+        def hidden_copy(dc, part):
             at = 0 if dc == 1 else 1
+            low, high = hidden_parts[part]
+            span = slice(low * LANES, high * LANES)
             return pltpu.make_async_remote_copy(
-                src_ref=hid,
-                dst_ref=hide.at[at],
-                send_sem=hidden_send.at[at],
-                recv_sem=hidden_recv.at[at],
+                src_ref=hid.at[:, span],
+                dst_ref=hide.at[at, :, span],
+                send_sem=hidden_send.at[at, part],
+                recv_sem=hidden_recv.at[at, part],
                 device_id=reach(0, dc)[1],
                 device_id_type=MESH,
             )
+
+        def hidden_start(*parts):
+            for part in parts:
+                for dc in (1, -1):
+                    pl.when(reach(0, dc)[0])(hidden_copy(dc, part).start)
+
+        def hidden_wait(*parts):
+            for part in parts:
+                for dc in (1, -1):
+                    pl.when(reach(0, -dc)[0])(hidden_copy(dc, part).wait_recv)
+
+        def bias_columns():
+            bias_load.wait()
+            return [
+                jnp.broadcast_to(bias[layer : layer + 1, :], (8, bias.shape[1])).T[:channels, 0:1]
+                for layer in range(2)
+            ]
+
+        def convolved(layer, fields, first, count):
+            products = jnp.dot(
+                taps(b, weights, layer), column_stack(b, *fields), preferred_element_type=F32
+            )
+            return row_sum(b, products, first, count)
+
+        def settle_hidden(raw, offset, first):
+            count = raw.shape[1] // LANES
+            row = lax.shift_right_logical(lane_index(count * LANES), cols.bit_length() - 1)
+            if b == 3:
+                row = jnp.where(row >= 6, row - 8, row)
+            else:
+                row = row + (first + HIDDEN_START[b] - before) * (LANES // cols)
+            low = jnp.where(place == 0, 0, -LANES)
+            high = jnp.where(place == row_count - 1, rows, 2 * LANES)
+            hidden = jnp.where((row >= low) & (row < high), jnp.maximum(raw + offset, 0.0), 0.0)
+            hid[:, first * LANES : (first + count) * LANES] = hidden.astype(BF16)
+
+        def hidden_tiles(offset, first, count):
+            low = max(first + HIDDEN_START[b] - 1, 0)
+            high = min(first + HIDDEN_START[b] + count + 1, FIELD_TILES[b])
+            span = slice(low * LANES, high * LANES)
+            fields = (own[:, span], side[0, :, span], side[1, :, span])
+            start = first + HIDDEN_START[b] - low
+            settle_hidden(convolved(0, fields, start, count), offset, first)
+
+        def settled_tiles(offset, first, count):
+            span = slice(first * LANES, (first + count + 2) * LANES)
+            fields = (hid[:, span], hide[0, :, span], hide[1, :, span])
+            after = convolved(1, fields, 1, count)
+            kept = own[:, (before + first) * LANES : (before + first + count) * LANES]
+            final = jnp.maximum(after + offset + kept.astype(F32), 0.0)
+            settled[:, first * LANES : (first + count) * LANES] = final.astype(BF16)
 
         def ends(strip, chunk):
             if b == 3:
@@ -315,10 +375,10 @@
             at = (strip * chunks + chunk) * size
             return settled.at[:, at : at + size], held.at[:, chunk * size : (chunk + 1) * size]
 
-        def exchange(here, closing=False):
+        def exchange(here, strips=(), handing=False, closing=False):
             count = 0
 
-            def send(source, target, arrived, device):
+            def send(source, target, arrived, device, act=True):
                 nonlocal count
                 copy = pltpu.make_async_remote_copy(
                     src_ref=source,
@@ -331,24 +391,28 @@
                 count += 1
                 if closing:
                     copy.wait_send()
-                else:
+                elif act:
                     copy.start()
 
             at_once = []
             for strip, chunk in own_pieces(b, here):
                 source, target = ends(strip, chunk)
+                act = strip in strips
                 if here == b and strip == here:
-                    if not closing:
-                        copy = pltpu.make_async_copy(source, target, own_sem.at[chunk])
+                    copy = pltpu.make_async_copy(source, target, own_sem.at[chunk])
+                    if act:
                         copy.start()
+                    if handing:
                         at_once.append(copy)
                     continue
                 via = route(b, here, strip, chunk)
                 if via is None:
-                    send(source, target, strip_recv.at[b], (here, strip, col))
+                    send(source, target, strip_recv.at[b], (here, strip, col), act)
                 else:
                     slot = relayed(b, via).index((here, strip, chunk))
-                    send(source, relay.at[slot], relay_recv.at[slot], (b, via, col))
+                    send(source, relay.at[slot], relay_recv.at[slot], (b, via, col), act)
+            if not handing and not closing:
+                return
             for slot, (tile, strip, chunk) in enumerate(relayed(b, here)):
                 piece = relay.at[slot]
                 if not closing:
@@ -389,57 +453,6 @@
                     region = halo_region(dr, dc)
                     region[...] = jnp.zeros(region.shape, BF16)
 
-            bias_load.wait()
-            offsets = [
-                jnp.broadcast_to(bias[layer : layer + 1, :], (8, bias.shape[1])).T[:channels, 0:1]
-                for layer in range(2)
-            ]
-            weight_loads[0].wait()
-            for dr, dc in order:
-                pl.when(reach(-dr, -dc)[0])(halo_copy(dr, dc).wait_recv)
-
-            fields = [own, side.at[0], side.at[1]]
-            if packed:
-                for at, dc in enumerate((0, 1, -1)):
-                    upper = pack_recv[WAYS.index((1, dc))].astype(F32)
-                    lower = pack_recv[WAYS.index((-1, dc))].astype(F32)
-                    lines = []
-                    for g in range(folds):
-                        span = slice(g * 96, (g + 1) * 96)
-                        here = fields[at][span, middle]
-                        above = turned(upper, LANES - pair - pair * g)
-                        if b == 3:
-                            ring = jnp.where(lane < 96, turned(lower, 64 - pair * g), above)
-                            lines.append(jnp.where(lane < 64, here.astype(F32), ring).astype(BF16))
-                        else:
-                            below = turned(lower, -pair * g)
-                            lines.append(
-                                jnp.concatenate([above.astype(BF16), here, below.astype(BF16)], axis=1)
-                            )
-                    fields[at] = jnp.concatenate(lines, axis=0)
-            else:
-                fields = [field[...] for field in fields]
-
-            products = jnp.dot(
-                taps(b, weights, 0),
-                column_stack(b, *fields),
-                preferred_element_type=F32,
-            )
-            first = 1 if b == 0 else 0
-            hidden = row_sum(b, products, first, HIDDEN_TILES[b])
-            hidden = jnp.maximum(hidden + offsets[0], 0.0)
-            row = lax.shift_right_logical(lane_index(HIDDEN_TILES[b] * LANES), cols.bit_length() - 1)
-            if b == 3:
-                row = jnp.where(row >= 6, row - 8, row)
-            else:
-                row = row - (before - first) * (LANES // cols)
-            low = jnp.where(place == 0, 0, -LANES)
-            high = jnp.where(place == row_count - 1, rows, 2 * LANES)
-            hidden = jnp.where((row >= low) & (row < high), hidden, 0.0)
-            hid[...] = hidden.astype(BF16)
-
-            for dc in (1, -1):
-                pl.when(reach(0, dc)[0])(hidden_copy(dc).start)
             for dc in (1, -1):
 
                 @pl.when(jnp.logical_not(reach(0, -dc)[0]))
@@ -447,15 +460,59 @@
                     at = 0 if dc == 1 else 1
                     hide[at] = jnp.zeros(hid.shape, BF16)
 
+            def halo_wait(ways):
+                for dr, dc in ways:
+                    pl.when(reach(-dr, -dc)[0])(halo_copy(dr, dc).wait_recv)
+
+            def leave(**how):
+                for here in range(STRIPS):
+                    pl.when(place == here)(partial(exchange, here, **how))
+
+            offsets = bias_columns()
+            weight_loads[0].wait()
+            if not packed:
+                size = tiles // STRIPS
+                halo_wait([way for way in order if not way[0]])
+                hidden_tiles(offsets[0], 2, last - 4)
+                hidden_start(0)
+                halo_wait([way for way in order if way[0]])
+                hidden_tiles(offsets[0], 0, 2)
+                hidden_tiles(offsets[0], last - 2, 2)
+                hidden_start(1, 2)
+                weight_loads[1].wait()
+                hidden_wait(0)
+                settled_tiles(offsets[1], size, 2 * size)
+                leave(strips=(1, 2))
+                hidden_wait(1)
+                settled_tiles(offsets[1], 0, size)
+                hidden_wait(2)
+                settled_tiles(offsets[1], 3 * size, size)
+                leave(strips=(0, 3), handing=True)
+                return
+
+            halo_wait(order)
+            fields = []
+            for target, dc in ((own, 0), (side.at[0], 1), (side.at[1], -1)):
+                upper = pack_recv[WAYS.index((1, dc))].astype(F32)
+                lower = pack_recv[WAYS.index((-1, dc))].astype(F32)
+                lines = []
+                for g in range(folds):
+                    here = target[g * 96 : (g + 1) * 96, middle]
+                    above = turned(upper, LANES - pair - pair * g)
+                    if b == 3:
+                        ring = jnp.where(lane < 96, turned(lower, 64 - pair * g), above)
+                        lines.append(jnp.where(lane < 64, here.astype(F32), ring).astype(BF16))
+                    else:
+                        below = turned(lower, -pair * g)
+                        lines.append(
+                            jnp.concatenate([above.astype(BF16), here, below.astype(BF16)], axis=1)
+                        )
+                fields.append(jnp.concatenate(lines, axis=0))
+            settle_hidden(convolved(0, fields, 0, last), offsets[0], 0)
+            hidden_start(0)
             weight_loads[1].wait()
-            for dc in (1, -1):
-                pl.when(reach(0, -dc)[0])(hidden_copy(dc).wait_recv)
-            products = jnp.dot(
-                taps(b, weights, 1),
-                column_stack(b, hid[...], hide[0], hide[1]),
-                preferred_element_type=F32,
-            )
-            after = row_sum(b, products, 1 if b == 0 else before, tiles)
+            hidden_wait(0)
+            after = convolved(1, (hid[...], hide[0], hide[1]), before, tiles)
             final = jnp.maximum(after + offsets[1] + own[:, middle].astype(F32), 0.0)
             if b < 3:
                 settled[...] = final.astype(BF16)
@@ -467,16 +524,16 @@
                         out = part if g == 0 else jnp.where(lane < 16 * g, out, part)
                     settled[strip] = out.astype(BF16)
 
-            for here in range(STRIPS):
-                pl.when(place == here)(partial(exchange, here))
+            leave(strips=range(STRIPS), handing=True)
 
         def close():
             for here in range(STRIPS):
-                pl.when(place == here)(partial(exchange, here, True))
+                pl.when(place == here)(partial(exchange, here, closing=True))
             for dr, dc in order:
                 pl.when(reach(dr, dc)[0])(halo_copy(dr, dc).wait_send)
-            for dc in (1, -1):
-                pl.when(reach(0, dc)[0])(hidden_copy(dc).wait_send)
+            for part in range(len(hidden_parts)):
+                for dc in (1, -1):
+                    pl.when(reach(0, dc)[0])(hidden_copy(dc, part).wait_send)
 
         return begin, run, close
 
@@ -650,8 +707,8 @@
     scratch += [pltpu.VMEM((STRIPS, WIDTH, LANES), BF16)]
     pieces = ((48, 256), (96, 128), (96, 128), (48, 128))
     scratch += [pltpu.VMEM((RELAYS, *piece), BF16) for piece in pieces]
-    counts = (6, 8, 8, 2, 2, 16 + RELAYS, 4, RELAYS, 4)
-    scratch += [pltpu.SemaphoreType.DMA((count,)) for count in counts]
+    counts = ((6,), (8,), (8,), (2, 3), (2, 3), (16 + RELAYS,), (4,), (RELAYS,), (4,))
+    scratch += [pltpu.SemaphoreType.DMA(count) for count in counts]
     return pl.pallas_call(
         front_kernel,
         out_shape=[pltpu.VMEM(shape, BF16) for shape in OUT_SHAPES],

time: 22.7 us -> 23.4 us (1.031)
  Pallas kernels: 21.9 us -> 22.7 us
    pallas_call x1, Pallas kernels: 21.2 us -> 22 us  [front(): pl.pallas_call(front_kernel, out_shape=[pltpu.VMEM(shape, BF16) for shape...]
where the time goes in v4:
time: 23.4 us; the launch traced here: 23.3 us
  Pallas kernels  22.7 us (97%)
  between operations  0.64 us (3%)
    pallas_call x1, Pallas kernels, front(): pl.pallas_call(front_kernel, out_shape=[pltpu.VMEM(shape, BF16) for shape...  22 us
    pallas_call x1, Pallas kernels, finished(): pl.pallas_call(finish_kernel, out_shape=[jax.ShapeDtypeStruct(out.shape,...  0.71 us

profile of v4, /device:TPU:24, one launch (start us, length us, event | category | flops | bytes accessed | tf_op | source)
XLA Modules:
  0.0 23.3 jit_solution(11465955122383422855)
XLA Ops:
  0.6 22.0 %front.1 = (bf16[48,8,128]{2,1,0:T(8,128)(2,1)S(1)}, bf16[256,96]{1,0:T(8,128)(2,1)S(1)}, bf16[64,192]{1,0:T(8,128)(2,1)S(1)}, bf16[16,384]{1,0:T(8,128)(2,1)S(1)}) custom-call(bf16[48,4096]{1,0:T(8,128)(2,1)} %bitcast.13, bf16[2,3,3,384,384]{4,3,2,1,0:T(8,128)(2,1)} %bitcast.12, f32[2,384]{1,0:T(2,128)} %bitcast.14, bf16[720,720]{1,0:T(8,128)(2,1)} %join_weight.1, ...), custom_call_target="tpu_custom_call" | custom-call | tf_op jit(solution)/shard_map/front/pallas_call | solution.py:712
  22.6 0.7 %finish.1 = (bf16[48,8,128]{2,1,0:T(8,128)(2,1)}, bf16[256,96]{1,0:T(8,128)(2,1)}, bf16[64,192]{1,0:T(8,128)(2,1)}, bf16[16,384]{1,0:T(8,128)(2,1)}) custom-call(bf16[48,8,128]{2,1,0:T(8,128)(2,1)S(1)} %get-tuple-element.12.refs_0_, bf16[256,96]{1,0:T(8,128)(2,1)S(1)} %get-tuple-element.13.refs_1_, bf16[64,192]{1,0:T(8,128)(2,1)S(1)} %get-tuple-element.14.refs_2_, ...), custom_call_target="tpu_custom_call" | custom-call | tf_op jit(solution)/shard_map/finish/pallas_call | solution.py:747

commit v5 on v4

--- a/solution.py
+++ b/solution.py
@@ -29,7 +29,7 @@
 
 
 def route(source, tile, strip, chunk):
-    if tile == source or strip == tile:
+    if tile == source or strip == tile or source >= 2:
         return None
     if source == 0 and strip == 3 - tile and chunk % 2 == 0:
         return None
@@ -214,7 +214,14 @@
     def _():
         pl.semaphore_signal(barrier, inc=1, device_id=(0, level, col), device_id_type=MESH)
 
+    for far in (2, 3):
+
+        @pl.when(jnp.logical_not(at_home & (level == far)))
+        def _():
+            pl.semaphore_signal(barrier, inc=1, device_id=(far, level, col), device_id_type=MESH)
+
     expected = expected + 2 * (STRIPS - 1) + ((level == 0) & (place > 0)).astype(jnp.int32)
+    expected = expected + jnp.where(level >= 2, STRIPS - at_home.astype(jnp.int32), 0)
 
     helds = (held0, held1, held2, held3)
     owns = (own0, own1, own2, own3)
@@ -428,7 +435,7 @@
             for copy in at_once:
                 copy.wait()
 
-        def run():
+        def open_halo():
             load.wait()
             if b:
                 own[:, middle] = natural_tile(b, container)
@@ -460,13 +467,16 @@
                     at = 0 if dc == 1 else 1
                     hide[at] = jnp.zeros(hid.shape, BF16)
 
+        def run():
             def halo_wait(ways):
                 for dr, dc in ways:
                     pl.when(reach(-dr, -dc)[0])(halo_copy(dr, dc).wait_recv)
 
-            def leave(**how):
+            def leave(early, **how):
                 for here in range(STRIPS):
-                    pl.when(place == here)(partial(exchange, here, **how))
+                    soon = [strip for strip in (1, 2) if strip != STRIPS - 1 - here]
+                    strips = soon if early else [s for s in range(STRIPS) if s not in soon or packed]
+                    pl.when(place == here)(partial(exchange, here, strips, **how))
 
             offsets = bias_columns()
             weight_loads[0].wait()
@@ -482,12 +492,12 @@
                 weight_loads[1].wait()
                 hidden_wait(0)
                 settled_tiles(offsets[1], size, 2 * size)
-                leave(strips=(1, 2))
+                leave(True)
                 hidden_wait(1)
                 settled_tiles(offsets[1], 0, size)
                 hidden_wait(2)
                 settled_tiles(offsets[1], 3 * size, size)
-                leave(strips=(0, 3), handing=True)
+                leave(False, handing=True)
                 return
 
             halo_wait(order)
@@ -524,7 +534,7 @@
                         out = part if g == 0 else jnp.where(lane < 16 * g, out, part)
                     settled[strip] = out.astype(BF16)
 
-            leave(strips=range(STRIPS), handing=True)
+            leave(False, handing=True)
 
         def close():
             for here in range(STRIPS):
@@ -535,17 +545,19 @@
                 for dc in (1, -1):
                     pl.when(reach(0, dc)[0])(hidden_copy(dc, part).wait_send)
 
-        return begin, run, close
+        return begin, open_halo, run, close
 
     branches = [branch(b) for b in range(STRIPS)]
-    for b, (begin, _, _) in enumerate(branches):
+    for b, (begin, _, _, _) in enumerate(branches):
         pl.when(level == b)(begin)
+    for b, (_, open_halo, _, _) in enumerate(branches):
+        pl.when(level == b)(open_halo)
 
     pool_refs = (pool0, pool1, pool2)
     for fine, pool in enumerate(pool_refs):
         pool[...] = pool_table(fine)
 
-    for b, (_, run, _) in enumerate(branches):
+    for b, (_, _, run, _) in enumerate(branches):
         pl.when(level == b)(run)
 
     for copy in mix_loads:
@@ -564,7 +576,7 @@
 
     join(place, arrived, helds, mix, mix_bias, pool_refs, (out0, out1, out2, out3))
 
-    for b, (_, _, close) in enumerate(branches):
+    for b, (_, _, _, close) in enumerate(branches):
         pl.when(level == b)(close)
 
 

time: 23.4 us -> 24.1 us (1.030)
  Pallas kernels: 22.7 us -> 23.3 us
    pallas_call x1, Pallas kernels: 22 us -> 22.6 us  [front(): pl.pallas_call(front_kernel, out_shape=[pltpu.VMEM(shape, BF16) for shape...]
where the time goes in v5:
time: 24.1 us; the launch traced here: 23.9 us
  Pallas kernels  23.3 us (97%)
  between operations  0.64 us (3%)
    pallas_call x1, Pallas kernels, front(): pl.pallas_call(front_kernel, out_shape=[pltpu.VMEM(shape, BF16) for shape...  22.6 us
    pallas_call x1, Pallas kernels, finished(): pl.pallas_call(finish_kernel, out_shape=[jax.ShapeDtypeStruct(out.shape,...  0.71 us

profile of v5, /device:TPU:24, one launch (start us, length us, event | category | flops | bytes accessed | tf_op | source)
XLA Modules:
  0.0 23.9 jit_solution(17218065444241064714)
XLA Ops:
  0.6 22.6 %front.1 = (bf16[48,8,128]{2,1,0:T(8,128)(2,1)S(1)}, bf16[256,96]{1,0:T(8,128)(2,1)S(1)}, bf16[64,192]{1,0:T(8,128)(2,1)S(1)}, bf16[16,384]{1,0:T(8,128)(2,1)S(1)}) custom-call(bf16[48,4096]{1,0:T(8,128)(2,1)} %bitcast.13, bf16[2,3,3,384,384]{4,3,2,1,0:T(8,128)(2,1)} %bitcast.12, f32[2,384]{1,0:T(2,128)} %bitcast.14, bf16[720,720]{1,0:T(8,128)(2,1)} %join_weight.1, ...), custom_call_target="tpu_custom_call" | custom-call | tf_op jit(solution)/shard_map/front/pallas_call | solution.py:724
  23.2 0.7 %finish.1 = (bf16[48,8,128]{2,1,0:T(8,128)(2,1)}, bf16[256,96]{1,0:T(8,128)(2,1)}, bf16[64,192]{1,0:T(8,128)(2,1)}, bf16[16,384]{1,0:T(8,128)(2,1)}) custom-call(bf16[48,8,128]{2,1,0:T(8,128)(2,1)S(1)} %get-tuple-element.12.refs_0_, bf16[256,96]{1,0:T(8,128)(2,1)S(1)} %get-tuple-element.13.refs_1_, bf16[64,192]{1,0:T(8,128)(2,1)S(1)} %get-tuple-element.14.refs_2_, ...), custom_call_target="tpu_custom_call" | custom-call | tf_op jit(solution)/shard_map/finish/pallas_call | solution.py:759

commit v6 on v5

--- a/solution.py
+++ b/solution.py
@@ -29,7 +29,7 @@
 
 
 def route(source, tile, strip, chunk):
-    if tile == source or strip == tile or source >= 2:
+    if tile == source or strip == tile or source == 3:
         return None
     if source == 0 and strip == 3 - tile and chunk % 2 == 0:
         return None
@@ -44,7 +44,19 @@
         for strip in range(STRIPS)
         if tile != place and route(source, tile, strip, chunk) == place
     ]
-    return sorted(pieces, key=lambda p: (p[2], (p[0] ^ place).bit_count(), -abs(p[0] - source)))
+    return sorted(
+        pieces,
+        key=lambda p: (
+            source == 0 and halo_bound(*p[1:]),
+            p[2],
+            (p[0] ^ place).bit_count(),
+            -abs(p[0] - source),
+        ),
+    )
+
+
+def halo_bound(strip, chunk):
+    return (strip, chunk) in ((0, 0), (STRIPS - 1, CHUNKS[0] - 1))
 
 
 def own_pieces(source, place):
@@ -214,14 +226,12 @@
     def _():
         pl.semaphore_signal(barrier, inc=1, device_id=(0, level, col), device_id_type=MESH)
 
-    for far in (2, 3):
-
-        @pl.when(jnp.logical_not(at_home & (level == far)))
-        def _():
-            pl.semaphore_signal(barrier, inc=1, device_id=(far, level, col), device_id_type=MESH)
-
+    @pl.when(jnp.logical_not(at_home & (level == 3)))
+    def _():
+        pl.semaphore_signal(barrier, inc=1, device_id=(3, level, col), device_id_type=MESH)
+
+    expected = expected + jnp.where(level == 3, STRIPS - at_home.astype(jnp.int32), 0)
     expected = expected + 2 * (STRIPS - 1) + ((level == 0) & (place > 0)).astype(jnp.int32)
-    expected = expected + jnp.where(level >= 2, STRIPS - at_home.astype(jnp.int32), 0)
 
     helds = (held0, held1, held2, held3)
     owns = (own0, own1, own2, own3)
@@ -382,7 +392,7 @@
             at = (strip * chunks + chunk) * size
             return settled.at[:, at : at + size], held.at[:, chunk * size : (chunk + 1) * size]
 
-        def exchange(here, strips=(), handing=False, closing=False):
+        def exchange(here, wanted=None, handing=False, closing=False):
             count = 0
 
             def send(source, target, arrived, device, act=True):
@@ -404,7 +414,7 @@
             at_once = []
             for strip, chunk in own_pieces(b, here):
                 source, target = ends(strip, chunk)
-                act = strip in strips
+                act = not closing and wanted(strip, chunk)
                 if here == b and strip == here:
                     copy = pltpu.make_async_copy(source, target, own_sem.at[chunk])
                     if act:
@@ -472,32 +482,38 @@
                 for dr, dc in ways:
                     pl.when(reach(-dr, -dc)[0])(halo_copy(dr, dc).wait_recv)
 
-            def leave(early, **how):
+            def leave(wanted, **how):
                 for here in range(STRIPS):
-                    soon = [strip for strip in (1, 2) if strip != STRIPS - 1 - here]
-                    strips = soon if early else [s for s in range(STRIPS) if s not in soon or packed]
-                    pl.when(place == here)(partial(exchange, here, strips, **how))
+                    pl.when(place == here)(partial(exchange, here, wanted, **how))
 
             offsets = bias_columns()
             weight_loads[0].wait()
+            def anything(strip, chunk):
+                return True
+
             if not packed:
-                size = tiles // STRIPS
                 halo_wait([way for way in order if not way[0]])
                 hidden_tiles(offsets[0], 2, last - 4)
                 hidden_start(0)
+                if b == 0:
+                    weight_loads[1].wait()
+                    hidden_wait(0)
+                    settled_tiles(offsets[1], 2, tiles - 4)
+                    leave(lambda strip, chunk: not halo_bound(strip, chunk))
                 halo_wait([way for way in order if way[0]])
                 hidden_tiles(offsets[0], 0, 2)
                 hidden_tiles(offsets[0], last - 2, 2)
                 hidden_start(1, 2)
-                weight_loads[1].wait()
-                hidden_wait(0)
-                settled_tiles(offsets[1], size, 2 * size)
-                leave(True)
-                hidden_wait(1)
-                settled_tiles(offsets[1], 0, size)
-                hidden_wait(2)
-                settled_tiles(offsets[1], 3 * size, size)
-                leave(False, handing=True)
+                if b == 0:
+                    hidden_wait(1, 2)
+                    settled_tiles(offsets[1], 0, 2)
+                    settled_tiles(offsets[1], tiles - 2, 2)
+                    leave(halo_bound, handing=True)
+                else:
+                    weight_loads[1].wait()
+                    hidden_wait(0, 1, 2)
+                    settled_tiles(offsets[1], 0, tiles)
+                    leave(anything, handing=True)
                 return
 
             halo_wait(order)
@@ -534,7 +550,7 @@
                         out = part if g == 0 else jnp.where(lane < 16 * g, out, part)
                     settled[strip] = out.astype(BF16)
 
-            leave(False, handing=True)
+            leave(anything, handing=True)
 
         def close():
             for here in range(STRIPS):
@@ -574,7 +590,12 @@
         )
         pl.when(jnp.logical_not(at_home & (level == source)))(arrival.wait_recv)
 
-    join(place, arrived, helds, mix, mix_bias, pool_refs, (out0, out1, out2, out3))
+    for late3 in (True, False):
+
+        @pl.when((level < 2) if late3 else (level >= 2))
+        def _():
+            outs = (out0, out1, out2, out3)
+            join(late3, place, arrived, helds, mix, mix_bias, pool_refs, outs)
 
     for b, (_, _, _, close) in enumerate(branches):
         pl.when(level == b)(close)
@@ -635,7 +656,7 @@
     )
 
 
-def join(place, arrived, helds, mix, mix_bias, pools, outs):
+def join(late3, place, arrived, helds, mix, mix_bias, pools, outs):
     lane = lane_index()
     total = mix_bias.shape[0]
     line = jnp.concatenate([mix_bias[...][None, :], jnp.zeros((1, -total % LANES), F32)], axis=1)
@@ -644,10 +665,18 @@
     offsets = [offset[starts[b] : starts[b + 1], 0:1] for b in range(STRIPS)]
     one, two, three = (slice(starts[b], starts[b + 1]) for b in range(1, STRIPS))
 
-    arrived(3)
-    folded = helds[3][...].astype(F32)
-    last = jnp.concatenate([turned(folded, -16 * g) for g in range(8)], axis=0)
-    from3 = product(mix, slice(0, starts[3]), 3, last.astype(BF16))
+    def side_by_side(near, far):
+        return jnp.where(lane < 64, near, jnp.where(lane < 80, turned(far, 64), 0.0))
+
+    def take3():
+        arrived(3)
+        folded = helds[3][...].astype(F32)
+        last = jnp.concatenate([turned(folded, -16 * g) for g in range(8)], axis=0)
+        return last, product(mix, slice(0, starts[3]), 3, last.astype(BF16))
+
+    first = slice(0, starts[1])
+    if not late3:
+        last, from3 = take3()
 
     arrived(2)
     pieces = helds[2][...].astype(F32)
@@ -655,11 +684,8 @@
     third16 = third.astype(BF16)
     from2 = product(mix, slice(0, starts[2]), 2, third16)
     shrunk = jnp.dot(third16, pools[2][...], preferred_element_type=F32)
-    total3 = last + offsets[3] + product(mix, three, 2, (shrunk * 0.25).astype(BF16))
-    total2 = third + offsets[2] + spread(from3[two], pools[2][...])
-
-    def side_by_side(near, far):
-        return jnp.where(lane < 64, near, jnp.where(lane < 80, turned(far, 64), 0.0))
+    total3 = offsets[3] + product(mix, three, 2, (shrunk * 0.25).astype(BF16))
+    total2 = third + offsets[2]
 
     arrived(1)
     second = helds[1][...]
@@ -670,11 +696,24 @@
     total2 = total2 + down1[: starts[3] - starts[2]]
     tail3 = down1[starts[3] - starts[2] :]
     total1 = second.astype(F32) + offsets[1]
-    total1 = total1 + spread(side_by_side(from2[one], from3[one]), pools[1][...])
-    first = slice(0, starts[1])
-    total0 = offsets[0] + spread(
-        jnp.concatenate([from1, side_by_side(from2[first], from3[first])], axis=1), pools[0][...]
-    )
+
+    def add3(total0, total1, total2, total3, far0, far1):
+        return (
+            total0 + spread(far0, pools[0][...]),
+            total1 + spread(far1, pools[1][...]),
+            total2 + spread(from3[two], pools[2][...]),
+            total3 + last,
+        )
+
+    if late3:
+        nothing = jnp.zeros((1, LANES), F32)
+        near0 = jnp.concatenate([from1, side_by_side(from2[first], nothing)], axis=1)
+        total0 = offsets[0] + spread(near0, pools[0][...])
+        total1 = total1 + spread(side_by_side(from2[one], nothing), pools[1][...])
+    else:
+        far0 = jnp.concatenate([from1, side_by_side(from2[first], from3[first])], axis=1)
+        far1 = side_by_side(from2[one], from3[one])
+        total0, total1, total2, total3 = add3(offsets[0], total1, total2, total3, far0, far1)
 
     arrived(0)
     maps = helds[0][...]
@@ -685,6 +724,13 @@
     down0 = product(mix, slice(starts[2], total), 0, far)
     total2 = total2 + down0[: starts[3] - starts[2]]
     total3 = total3 + turned(tail3 + down0[starts[3] - starts[2] :], -64)
+    if late3:
+        last, from3 = take3()
+        apart = jnp.where((lane >= 64) & (lane < 80), turned(from3[: starts[2]], 64), 0.0)
+        total0 = total0 + spread(apart[first], pools[0][:, 256:])
+        total1 = total1 + spread(apart[one], pools[1][...])
+        total2 = total2 + spread(from3[two], pools[2][...])
+        total3 = total3 + last
     total0 = jnp.maximum(total0 + maps.astype(F32), 0.0)
     lines = [total0[:, at : at + LANES] for at in range(0, total0.shape[1], LANES)]
     outs[0][...] = jnp.stack(lines, axis=1).astype(BF16)

time: 24.1 us -> 21.5 us (0.89)
  Pallas kernels: 23.3 us -> 20.7 us
    pallas_call x1, Pallas kernels: 22.6 us -> 20 us  [front(): pl.pallas_call(front_kernel, out_shape=[pltpu.VMEM(shape, BF16) for shape...]
where the time goes in v6:
time: 21.5 us; the launch traced here: 21.3 us
  Pallas kernels  20.7 us (96%)
  between operations  0.64 us (3%)
    pallas_call x1, Pallas kernels, front(): pl.pallas_call(front_kernel, out_shape=[pltpu.VMEM(shape, BF16) for shape...  20 us
    pallas_call x1, Pallas kernels, finished(): pl.pallas_call(finish_kernel, out_shape=[jax.ShapeDtypeStruct(out.shape,...  0.71 us

profile of v6, /device:TPU:24, one launch (start us, length us, event | category | flops | bytes accessed | tf_op | source)
XLA Modules:
  0.0 21.3 jit_solution(670359070218017474)
XLA Ops:
  0.6 20.0 %front.1 = (bf16[48,8,128]{2,1,0:T(8,128)(2,1)S(1)}, bf16[256,96]{1,0:T(8,128)(2,1)S(1)}, bf16[64,192]{1,0:T(8,128)(2,1)S(1)}, bf16[16,384]{1,0:T(8,128)(2,1)S(1)}) custom-call(bf16[48,4096]{1,0:T(8,128)(2,1)} %bitcast.13, bf16[2,3,3,384,384]{4,3,2,1,0:T(8,128)(2,1)} %bitcast.12, f32[2,384]{1,0:T(2,128)} %bitcast.14, bf16[720,720]{1,0:T(8,128)(2,1)} %join_weight.1, ...), custom_call_target="tpu_custom_call" | custom-call | tf_op jit(solution)/shard_map/front/pallas_call | solution.py:770
  20.6 0.7 %finish.1 = (bf16[48,8,128]{2,1,0:T(8,128)(2,1)}, bf16[256,96]{1,0:T(8,128)(2,1)}, bf16[64,192]{1,0:T(8,128)(2,1)}, bf16[16,384]{1,0:T(8,128)(2,1)}) custom-call(bf16[48,8,128]{2,1,0:T(8,128)(2,1)S(1)} %get-tuple-element.12.refs_0_, bf16[256,96]{1,0:T(8,128)(2,1)S(1)} %get-tuple-element.13.refs_1_, bf16[64,192]{1,0:T(8,128)(2,1)S(1)} %get-tuple-element.14.refs_2_, ...), custom_call_target="tpu_custom_call" | custom-call | tf_op jit(solution)/shard_map/finish/pallas_call | solution.py:805

commit v7 on v6

--- a/solution.py
+++ b/solution.py
@@ -24,14 +24,14 @@
 HIDDEN_START = (1, 0, 0, 0)
 
 
-CHUNKS = (4, 2, 2, 1)
+CHUNKS = (4, 2, 1, 1)
 RELAYS = 12
 
 
 def route(source, tile, strip, chunk):
     if tile == source or strip == tile or source == 3:
         return None
-    if source == 0 and strip == 3 - tile and chunk % 2 == 0:
+    if source == 0 and strip == 3 - tile and (chunk % 2 == 0 or strip == 0):
         return None
     return strip
 
@@ -381,13 +381,8 @@
             settled[:, first * LANES : (first + count) * LANES] = final.astype(BF16)
 
         def ends(strip, chunk):
-            if b == 3:
+            if packed:
                 return settled.at[strip], held
-            if b == 2:
-                size = channels // chunks
-                span = slice(chunk * size, (chunk + 1) * size)
-                tile = strip // 2
-                return settled.at[span, tile * LANES : (tile + 1) * LANES], held.at[span]
             size = tiles * LANES // STRIPS // chunks
             at = (strip * chunks + chunk) * size
             return settled.at[:, at : at + size], held.at[:, chunk * size : (chunk + 1) * size]
@@ -540,15 +535,16 @@
             hidden_wait(0)
             after = convolved(1, (hid[...], hide[0], hide[1]), before, tiles)
             final = jnp.maximum(after + offsets[1] + own[:, middle].astype(F32), 0.0)
-            if b < 3:
-                settled[...] = final.astype(BF16)
-            else:
-                for strip in range(STRIPS):
-                    out = None
-                    for g in range(8):
-                        part = turned(final[g * WIDTH : (g + 1) * WIDTH], 16 * g - 16 * strip)
-                        out = part if g == 0 else jnp.where(lane < 16 * g, out, part)
-                    settled[strip] = out.astype(BF16)
+            size = settled.shape[1]
+            pixels = strip_pixels(b)
+            for strip in range(STRIPS):
+                tile, at = divmod(strip * pixels, LANES)
+                strip_tile = final[:, tile * LANES : (tile + 1) * LANES]
+                out = None
+                for g in range(LANES // pixels):
+                    part = turned(strip_tile[g * size : (g + 1) * size], pixels * g - at)
+                    out = part if g == 0 else jnp.where(lane < pixels * g, out, part)
+                settled[strip] = out.astype(BF16)
 
             leave(anything, handing=True)
 
@@ -680,7 +676,7 @@
 
     arrived(2)
     pieces = helds[2][...].astype(F32)
-    third = jnp.where(lax.rem(place, 2) == 1, turned(pieces, 64), pieces)
+    third = jnp.concatenate([pieces, turned(pieces, -64)], axis=0)
     third16 = third.astype(BF16)
     from2 = product(mix, slice(0, starts[2]), 2, third16)
     shrunk = jnp.dot(third16, pools[2][...], preferred_element_type=F32)
@@ -738,7 +734,7 @@
         out[...] = jnp.maximum(value, 0.0).T[: out.shape[0]].astype(BF16)
 
 
-HELD_SHAPES = ((48, 1024), (96, 256), (192, 128), (48, 128))
+HELD_SHAPES = ((48, 1024), (96, 256), (96, 128), (48, 128))
 
 
 def front(section, kernels, biases, join_weight, join_bias):
@@ -761,8 +757,8 @@
     scratch += [pltpu.VMEM((2, 96, LANES), BF16), pltpu.VMEM((8, 96, LANES), BF16)]
     scratch += [pltpu.VMEM((2, *field(b, HIDDEN_TILES)), BF16) for b in range(4)]
     scratch += [pltpu.VMEM(field(b, HIDDEN_TILES), BF16) for b in range(4)]
-    scratch += [pltpu.VMEM(field(b, OWN_TILES), BF16) for b in range(3)]
-    scratch += [pltpu.VMEM((STRIPS, WIDTH, LANES), BF16)]
+    scratch += [pltpu.VMEM(field(b, OWN_TILES), BF16) for b in range(2)]
+    scratch += [pltpu.VMEM((STRIPS, size, LANES), BF16) for size in (2 * WIDTH, WIDTH)]
     pieces = ((48, 256), (96, 128), (96, 128), (48, 128))
     scratch += [pltpu.VMEM((RELAYS, *piece), BF16) for piece in pieces]
     counts = ((6,), (8,), (8,), (2, 3), (2, 3), (16 + RELAYS,), (4,), (RELAYS,), (4,))

time: 21.5 us -> 21 us (0.977)
  the two profiles are of different devices: /device:TPU:24 before, /device:TPU:23 now
where the time goes in v7:
time: 21 us; the launch traced here: 20.9 us
  Pallas kernels  20.3 us (97%)
  between operations  0.64 us (3%)
    pallas_call x1, Pallas kernels, front(): pl.pallas_call(front_kernel, out_shape=[pltpu.VMEM(shape, BF16) for shape...  19.5 us
    pallas_call x1, Pallas kernels, finished(): pl.pallas_call(finish_kernel, out_shape=[jax.ShapeDtypeStruct(out.shape,...  0.71 us

profile of v7, /device:TPU:23, one launch (start us, length us, event | category | flops | bytes accessed | tf_op | source)
XLA Modules:
  0.0 20.9 jit_solution(17571910464049508382)
XLA Ops:
  0.6 19.5 %front.1 = (bf16[48,8,128]{2,1,0:T(8,128)(2,1)S(1)}, bf16[256,96]{1,0:T(8,128)(2,1)S(1)}, bf16[64,192]{1,0:T(8,128)(2,1)S(1)}, bf16[16,384]{1,0:T(8,128)(2,1)S(1)}) custom-call(bf16[48,4096]{1,0:T(8,128)(2,1)} %bitcast.13, bf16[2,3,3,384,384]{4,3,2,1,0:T(8,128)(2,1)} %bitcast.12, f32[2,384]{1,0:T(2,128)} %bitcast.14, bf16[720,720]{1,0:T(8,128)(2,1)} %join_weight.1, ...), custom_call_target="tpu_custom_call" | custom-call | tf_op jit(solution)/shard_map/front/pallas_call | solution.py:766
  20.2 0.7 %finish.1 = (bf16[48,8,128]{2,1,0:T(8,128)(2,1)}, bf16[256,96]{1,0:T(8,128)(2,1)}, bf16[64,192]{1,0:T(8,128)(2,1)}, bf16[16,384]{1,0:T(8,128)(2,1)}) custom-call(bf16[48,8,128]{2,1,0:T(8,128)(2,1)S(1)} %get-tuple-element.12.refs_0_, bf16[256,96]{1,0:T(8,128)(2,1)S(1)} %get-tuple-element.13.refs_1_, bf16[64,192]{1,0:T(8,128)(2,1)S(1)} %get-tuple-element.14.refs_2_, ...), custom_call_target="tpu_custom_call" | custom-call | tf_op jit(solution)/shard_map/finish/pallas_call | solution.py:801

commit v8 on v7

--- a/solution.py
+++ b/solution.py
@@ -31,7 +31,7 @@
 def route(source, tile, strip, chunk):
     if tile == source or strip == tile or source == 3:
         return None
-    if source == 0 and strip == 3 - tile and (chunk % 2 == 0 or strip == 0):
+    if source == 0 and strip == 3 - tile:
         return None
     return strip
 
@@ -456,7 +456,7 @@
                     pack_send[end] = out.astype(BF16)
 
             pl.semaphore_wait(barrier, expected)
-            for dr, dc in order:
+            for dr, dc in sorted(order, key=lambda way: way[0] != 0):
                 pl.when(reach(dr, dc)[0])(halo_copy(dr, dc).start)
             for dr, dc in order:
 

time: 21 us -> 21.1 us (level)
  no operation moved by 1% of the time
where the time goes in v8:
time: 21.1 us; the launch traced here: 20.9 us
  Pallas kernels  20.3 us (96%)
  between operations  0.64 us (3%)
    pallas_call x1, Pallas kernels, front(): pl.pallas_call(front_kernel, out_shape=[pltpu.VMEM(shape, BF16) for shape...  19.6 us
    pallas_call x1, Pallas kernels, finished(): pl.pallas_call(finish_kernel, out_shape=[jax.ShapeDtypeStruct(out.shape,...  0.71 us

profile of v8, /device:TPU:23, one launch (start us, length us, event | category | flops | bytes accessed | tf_op | source)
XLA Modules:
  0.0 20.9 jit_solution(14909126890406179185)
XLA Ops:
  0.6 19.6 %front.1 = (bf16[48,8,128]{2,1,0:T(8,128)(2,1)S(1)}, bf16[256,96]{1,0:T(8,128)(2,1)S(1)}, bf16[64,192]{1,0:T(8,128)(2,1)S(1)}, bf16[16,384]{1,0:T(8,128)(2,1)S(1)}) custom-call(bf16[48,4096]{1,0:T(8,128)(2,1)} %bitcast.13, bf16[2,3,3,384,384]{4,3,2,1,0:T(8,128)(2,1)} %bitcast.12, f32[2,384]{1,0:T(2,128)} %bitcast.14, bf16[720,720]{1,0:T(8,128)(2,1)} %join_weight.1, ...), custom_call_target="tpu_custom_call" | custom-call | tf_op jit(solution)/shard_map/front/pallas_call | solution.py:766
  20.2 0.7 %finish.1 = (bf16[48,8,128]{2,1,0:T(8,128)(2,1)}, bf16[256,96]{1,0:T(8,128)(2,1)}, bf16[64,192]{1,0:T(8,128)(2,1)}, bf16[16,384]{1,0:T(8,128)(2,1)}) custom-call(bf16[48,8,128]{2,1,0:T(8,128)(2,1)S(1)} %get-tuple-element.12.refs_0_, bf16[256,96]{1,0:T(8,128)(2,1)S(1)} %get-tuple-element.13.refs_1_, bf16[64,192]{1,0:T(8,128)(2,1)S(1)} %get-tuple-element.14.refs_2_, ...), custom_call_target="tpu_custom_call" | custom-call | tf_op jit(solution)/shard_map/finish/pallas_call | solution.py:801
